TPU v7x, 32 devices: a whole 2x2x4 slice. The times are simulated.
32 devices in a mesh: gx: 8 (over z, y), gy: 4 (over x, core).
Axes of the slice: x: 2, y: 2, z: 4, core: 2. Of those that a mesh axis runs over, the one named last changes fastest.
Arguments:
- preserved_vector: float32 [14, 64, 32, 128], P(None, 'gx', 'gy'), may hold values from -200 to 200, as said below
- nasa_table: float32 [32, 6], replicated, may hold values from -4 to 4.5, as said below
- gas_constant: float32 [32], replicated, may hold values from 0.3 to 3
- species_index: int32 [9], replicated, may hold values from 0 to 31, as said below
- face_kind: int32 [8, 4, 2], P('gx', 'gy'), may hold values from 0 to 1
Outputs:
- increment: float32 [14, 64, 32, 128], P(None, 'gx', 'gy')
Inputs may be any that keep to these rules, and one draw needn't show every extreme that they name: `preserved_vector`: every cell is a physical state: positive partial densities and an energy whose temperature lies between 0.5 and 2.5. `nasa_table`: each row's cp over R polynomial exceeds 1.5 for temperatures 0.3 to 3. `species_index`: 9 distinct rows.
All inputs are finite; a program needn't handle non-finite values.
Results may differ from a plain program's by a relative error of at most 0.0003.
Values sent between devices are 32-bit elements; how exact they have to be, the bound alone decides.
A program may use at most 64 MiB of HBM per device.

v0:
```python
import functools

import jax
import jax.numpy as jnp
from jax import lax
from jax.experimental import pallas as pl
from jax.experimental.pallas import tpu as pltpu
from jax.sharding import PartitionSpec as P

NS = 9
NVAR = 14
EPSILON = 1e-06
COURANT = 0.8
TOTAL = NVAR
PRIMS = 24
VEL, PASSIVE, GAMMA, SOUND, SLOPES = 9, 12, 13, 14, 15
TABLE = 7 * NS


def fill_table(nasa_ref, gas_ref, index_ref, table_ref):
    for i in range(NS):
        row = index_ref[i]
        gas = gas_ref[row]
        values = [
            gas,
            gas * nasa_ref[5, row],
            gas * (nasa_ref[0, row] - 1.0),
            gas * nasa_ref[1, row] * (1.0 / 2.0),
            gas * nasa_ref[2, row] * (1.0 / 3.0),
            gas * nasa_ref[3, row] * (1.0 / 4.0),
            gas * nasa_ref[4, row] * (1.0 / 5.0),
        ]
        for n, value in enumerate(values):
            table_ref[n * NS + i] = jnp.full(table_ref.shape[1:], value, jnp.float32)


def tree(terms):
    terms = list(terms)
    while len(terms) > 1:
        terms = [a + b for a, b in zip(terms[::2], terms[1::2])] + (
            [terms[-1]] if len(terms) % 2 else []
        )
    return terms[0]


def thermo(u, table_ref):
    rho = tree(u[:NS])
    inverse = 1.0 / rho
    vel = [m * inverse for m in u[NS : NS + 3]]
    square = tree([v * v for v in vel])
    inner = u[NS + 3] - 0.5 * tree([v * m for v, m in zip(vel, u[NS : NS + 3])])
    mix = [tree([u[i] * table_ref[n * NS + i] for i in range(NS)]) for n in range(7)]
    gas, m6, m1, m2, m3, m4, m5 = mix
    c2, c3, c4, c5 = 2.0 * m2, 3.0 * m3, 4.0 * m4, 5.0 * m5
    temp = 1.0 - (tree([m6, m1, m2, m3, m4, m5]) - inner) / tree([m1, c2, c3, c4, c5])

    def heat(t):
        return m1 + t * (c2 + t * (c3 + t * (c4 + t * c5)))

    energy = m6 + temp * (m1 + temp * (m2 + temp * (m3 + temp * (m4 + temp * m5))))
    temp = temp - (energy - inner) / heat(temp)
    pressure = temp * gas
    gamma = gas / heat(temp)
    sound = jnp.sqrt((1.0 + gamma) * pressure * inverse)
    return inverse, vel, square, temp, pressure, gamma, sound


def slopes_of(temp, gamma, square, table_ref):
    kinetic = 0.5 * gamma * square
    result = []
    for i in range(NS):
        k = [table_ref[n * NS + i] for n in range(7)]
        e = k[1] + temp * (k[2] + temp * (k[3] + temp * (k[4] + temp * (k[5] + temp * k[6]))))
        result.append(k[0] * temp - gamma * e + kinetic)
    return result


def reciprocal(x):
    return pl.reciprocal(x, approx=True)


def correction(d):
    d0, d1, d2, d3 = d
    e0, e1, e2 = d1 - d0, d2 - d1, d3 - d2
    h1, h2 = 0.75 * d1, 0.75 * d2
    near, far = h1 * d1 + 0.75 * EPSILON, h2 * d2 + 0.75 * EPSILON
    r0 = reciprocal(e0 * (e0 + h1) + near)
    r1 = reciprocal(e1 * (e1 + h1) + near)
    r2 = reciprocal(e2 * (e2 - h2) + far)
    a = r0 * r0 * (1.0 / 3.0)
    b = r1 * r1
    c = r2 * r2
    g0, g2 = e0 - e1, e1 - e2
    return (a * (g0 + g0) + c * g2) * reciprocal(a + c + (b + b))


def face(normal, up, down, mean, linear, put):
    phi = [mean(SLOPES + i) for i in range(NS)]
    vel = [mean(VEL + i) for i in range(3)]
    gamma, sound = mean(GAMMA), mean(SOUND)
    inv = 1.0 / sound
    inv2, half_inv = inv * inv, 0.5 * inv
    tangents = [t for t in range(3) if t != normal]
    sigma, slow, fast = ([], []), ([], []), ([], [])
    shear = [([], []), ([], [])]
    for side, get in enumerate((up, down)):
        for k in range(4):
            s = get(TOTAL, k)
            m = [get(NS + i, k) for i in range(3)]
            dp = tree([phi[i] * get(i, k) for i in range(NS)]) + gamma * (
                get(NS + 3, k) - tree([vel[i] * m[i] for i in range(3)])
            )
            scaled = dp * inv2
            jump = (m[normal] - vel[normal] * s) * half_inv
            half = 0.5 * scaled
            sigma[side].append(scaled)
            slow[side].append(half - jump)
            fast[side].append(half + jump)
            for n, t in enumerate(tangents):
                shear[n][side].append(m[t] - vel[t] * s)

    def both(pair):
        return correction(pair[0]) - correction(pair[1])

    slower, faster = both(slow), both(fast)
    shears = [both(pair) for pair in shear]
    acoustic = slower + faster
    total, weighted, blend = None, None, None
    for i in range(NS):
        y = mean(i)
        amp = both(
            (
                [up(i, k) - y * sigma[0][k] for k in range(4)],
                [down(i, k) - y * sigma[1][k] for k in range(4)],
            )
        )
        put(i, linear(i) + y * acoustic + amp)
        total = amp if i == 0 else total + amp
        weighted = phi[i] * amp if i == 0 else weighted + phi[i] * amp
        blend = phi[i] * y if i == 0 else blend + phi[i] * y
    z = mean(PASSIVE)
    amp = both(
        (
            [up(NS + 4, k) - z * sigma[0][k] for k in range(4)],
            [down(NS + 4, k) - z * sigma[1][k] for k in range(4)],
        )
    )
    put(NS + 4, linear(NS + 4) + z * acoustic + amp)
    mass = acoustic + total
    swing = sound * (faster - slower)
    put(NS + normal, linear(NS + normal) + vel[normal] * mass + swing)
    for n, t in enumerate(tangents):
        put(NS + t, linear(NS + t) + vel[t] * mass + shears[n])
    square = tree([v * v for v in vel])
    energy = (
        square * mass
        + ((sound * sound - blend) * acoustic - weighted) / gamma
        + vel[normal] * swing
        + vel[tangents[0]] * shears[0]
        + vel[tangents[1]] * shears[1]
    )
    put(NS + 3, linear(NS + 3) + energy)


def fill_cells(u, i, table_ref, prim_ref):
    inverse, vel, square, temp, pressure, gamma, sound = thermo(u, table_ref)
    for k in range(NS):
        prim_ref[k, i] = u[k] * inverse
    for k in range(3):
        prim_ref[VEL + k, i] = vel[k]
    prim_ref[PASSIVE, i] = u[NS + 4] * inverse
    prim_ref[GAMMA, i] = gamma
    prim_ref[SOUND, i] = sound
    for k, value in enumerate(slopes_of(temp, gamma, square, table_ref)):
        prim_ref[SLOPES + k, i] = value
    prim_ref[PRIMS, i] = pressure


def fill_split(u, i, normal, alpha, prim_ref, up_ref, down_ref):
    speed = prim_ref[VEL + normal, i]
    push = 0.5 * prim_ref[PRIMS, i]
    half = 0.5 * speed
    lean = 0.5 * alpha
    plus, minus = half + lean, half - lean
    for ref, factor in ((up_ref, plus), (down_ref, minus)):
        for k in range(NVAR):
            value = u[k] * factor
            if k == NS + normal:
                value = value + push
            if k == NS + 3:
                value = value + push * speed
            ref[k, i] = value
        ref[TOTAL, i] = tree(u[:NS]) * factor


MESH = pl.DeviceIdType.MESH


def fused(
    size_x, size_y,
    nasa_ref, gas_ref, index_ref, kind_ref, flat_ref, planes_ref, source_ref, out_ref,
    x_ref, hx_ref, hy_ref, mine_ref, line_ref, slots_y, slots_x,
    table_ref, prim_ref, turn_ref, up_ref, down_ref, dup_ref, ddown_ref,
    fx_ref, fz_ref, acc_ref, edge_ref, fy_ref, s0_ref, s1_ref, s2_ref, s3_ref,
    load_sem, small_send, recv_y, recv_x, big_send, big_recv,
):
    load = pltpu.make_async_copy(flat_ref, x_ref, load_sem)
    load.start()
    gx, gy = lax.axis_index("gx"), lax.axis_index("gy")
    nx, ny = planes_ref.shape[1], planes_ref.shape[2]

    def along_x(offset):
        return (lax.rem(gx + offset, size_x), gy)

    def along_y(offset):
        return (gx, lax.rem(gy + offset, size_y))

    barrier = pltpu.get_barrier_semaphore()
    for n, along in ((size_x, along_x), (size_y, along_y)):
        for offset in range(1, n):
            pl.semaphore_signal(barrier, inc=1, device_id=along(offset), device_id_type=MESH)
    fill_table(nasa_ref, gas_ref, index_ref, table_ref)
    pl.semaphore_wait(barrier, size_x + size_y - 2)

    halos = []
    for n, (source, target, device) in enumerate(
        (
            (planes_ref.at[:, pl.ds(nx - 3, 3)], hx_ref.at[0], along_x(1)),
            (planes_ref.at[:, pl.ds(0, 3)], hx_ref.at[1], along_x(size_x - 1)),
            (source_ref.at[:, :, pl.ds(ny - 3, 3)], hy_ref.at[0], along_y(1)),
            (source_ref.at[:, :, pl.ds(0, 3)], hy_ref.at[1], along_y(size_y - 1)),
        )
    ):
        copy = pltpu.make_async_remote_copy(
            src_ref=source,
            dst_ref=target,
            send_sem=big_send.at[n],
            recv_sem=big_recv.at[n],
            device_id=device,
            device_id_type=MESH,
        )
        copy.start()
        halos.append(copy)
    load.wait()

    lanes = x_ref.shape[1]
    tile = (8, lanes)
    block = nx * ny

    def own(r, x):
        return x_ref[pl.ds(pl.multiple_of(r * block + x * 8, 8), 8), :]

    def turned(r, y):
        return x_ref[pl.ds(r * block + y, 8, stride=8), :]

    def differences(first, last, split):
        up_ref, down_ref, dup_ref, ddown_ref = split

        def step(i, _):
            for k in range(NVAR + 1):
                dup_ref[k, i] = up_ref[k, i + 1] - up_ref[k, i]
                ddown_ref[k, i] = down_ref[k, i + 1] - down_ref[k, i]
            return 0

        lax.fori_loop(first, last, step, 0)

    def faces_across(normal, first, last, prim_ref, split, flux_ref):
        up_ref, down_ref, dup_ref, ddown_ref = split

        def step(i, _):
            def linear(r):
                here = up_ref[r, i + 2] + down_ref[r, i + 3]
                ahead = dup_ref[r, i + 2] - ddown_ref[r, i + 2]
                return 6.0 * here + (ahead + ahead) + (dup_ref[r, i + 1] - ddown_ref[r, i + 3])

            def put(r, value):
                flux_ref[r, i] = value

            face(
                normal,
                lambda r, k: dup_ref[r, i + k],
                lambda r, k: ddown_ref[r, i + 4 - k],
                lambda q: 0.5 * (prim_ref[q, i + 2] + prim_ref[q, i + 3]),
                linear,
                put,
            )
            return 0

        lax.fori_loop(first, last, step, 0)

    def y_halo_tile(side, r, k):
        return hy_ref[side, r, :, k, 0, :]

    def cells_halo(normal, prims, split, read):
        def step(k, _):
            for side, base in ((0, 0), (1, 11)):
                u = [read(side, r, k) for r in range(NVAR)]
                fill_cells(u, k + base, table_ref, prims)
                fill_split(u, k + base, normal, alphas[normal], prims, *split[:2])
            return 0

        lax.fori_loop(0, 3, step, 0)

    def split_own(normal, prims, split, read):
        def step(n, _):
            u = [read(r, n) for r in range(NVAR)]
            fill_split(u, n + 3, normal, alphas[normal], prims, *split[:2])
            return 0

        lax.fori_loop(0, 8, step, 0)

    def y_prims(y, _):
        fill_cells([turned(r, y) for r in range(NVAR)], y + 3, table_ref, turn_ref)
        return 0

    lane = lax.broadcasted_iota(jnp.int32, tile, 1)

    width = 16
    spot = lane % width
    reach = spot - 3
    low_wall, high_wall = kind_ref[0] == 1, kind_ref[1] == 1
    low = jnp.where(reach < 0, jnp.where(low_wall, -1 - reach, 0), reach)
    beyond = spot - 13
    high = jnp.where(
        beyond >= 0,
        jnp.where(high_wall, lanes - 1 - beyond, lanes - 1),
        lanes + beyond,
    )
    source = jnp.where(spot < 8, low, high)
    mirrored = ((spot < 3) & low_wall) | ((spot > 12) & high_wall)
    sign = jnp.where(mirrored, -1.0, 1.0)
    group = lane // width

    def gather(values, index):
        return jnp.take_along_axis(values, index, axis=1)

    def z_edge(x, _):
        for r in range(NVAR):
            value = gather(own(r, x), source)
            if r == NS + 2:
                value = value * sign
            edge_ref[r] = jnp.where(group == x, value, edge_ref[r])
        return 0

    def roll(values, shift):
        return values if shift % lanes == 0 else pltpu.roll(values, shift % lanes, 1)

    def z_split(u, i):
        fill_split(u, i, 2, alphas[2], prim_ref, up_ref, down_ref)
        for k in range(NVAR + 1):
            dup_ref[k, i] = roll(up_ref[k, i], -1) - up_ref[k, i]
            ddown_ref[k, i] = roll(down_ref[k, i], -1) - down_ref[k, i]

    def z_own(x, _):
        u = [own(r, x) for r in range(NVAR)]
        z_split(u, x + 3)
        return 0

    def z_faces(x, _):
        i = jnp.where(x == 8, 14, x + 3)

        def linear(r):
            here = up_ref[r, i] + roll(down_ref[r, i], -1)
            ahead = dup_ref[r, i] - ddown_ref[r, i]
            return 6.0 * here + (ahead + ahead) + (
                roll(dup_ref[r, i], 1) - roll(ddown_ref[r, i], -1)
            )

        def mean(q):
            value = prim_ref[q, i]
            return 0.5 * (value + roll(value, -1))

        def put(r, value):
            fz_ref[r, x] = value

        face(
            2,
            lambda r, k: roll(dup_ref[r, i], 2 - k),
            lambda r, k: roll(ddown_ref[r, i], k - 2),
            mean,
            linear,
            put,
        )
        return 0

    def x_prims(x, best):
        u = [own(r, x) for r in range(NVAR)]
        fill_cells(u, x + 3, table_ref, prim_ref)
        sound = prim_ref[SOUND, x + 3]
        return tuple(
            jnp.maximum(b, jnp.abs(prim_ref[VEL + d, x + 3]) + sound) for d, b in enumerate(best)
        )

    zero = jnp.zeros(tile, jnp.float32)
    best = lax.fori_loop(0, 8, x_prims, (zero, zero, zero))
    best = [jnp.max(b, axis=(0, 1), keepdims=True) for b in best]
    row = lax.broadcasted_iota(jnp.int32, tile, 0)
    value = jnp.where(row == 0, best[0], jnp.where(row == 1, best[1], best[2]))

    def fill_turned():
        lax.fori_loop(0, 8, y_prims, 0)

    def fill_edge():
        for r in range(NVAR):
            edge_ref[r] = zero
        lax.fori_loop(0, 8, z_edge, 0)
        fill_cells([edge_ref[r] for r in range(NVAR)], 14, table_ref, prim_ref)

    for n, along, held, slots, recv, base, meanwhile in (
        (size_y, along_y, mine_ref, slots_y, recv_y, 0, fill_edge),
        (size_x, along_x, line_ref, slots_x, recv_x, size_y, fill_turned),
    ):
        held[...] = value
        copies = []
        for offset in range(1, n):
            copy = pltpu.make_async_remote_copy(
                src_ref=held,
                dst_ref=slots.at[offset],
                send_sem=small_send.at[base + offset],
                recv_sem=recv.at[offset],
                device_id=along(offset),
                device_id_type=MESH,
            )
            copy.start()
            copies.append(copy)
        meanwhile()
        for offset, copy in enumerate(copies, 1):
            copy.wait()
            value = jnp.maximum(value, slots[offset])
    alphas = [jnp.broadcast_to(value[d : d + 1], tile) for d in range(3)]

    z_split([edge_ref[r] for r in range(NVAR)], 14)
    lax.fori_loop(0, 8, z_own, 0)
    lax.fori_loop(0, 9, z_faces, 0)

    splits = (up_ref, down_ref, dup_ref, ddown_ref), (s0_ref, s1_ref, s2_ref, s3_ref)
    plans = (
        (1, turn_ref, splits[1], turned, y_halo_tile, fy_ref, halos[2:]),
        (0, prim_ref, splits[0], own, lambda side, r, k: hx_ref[side, r, k], fx_ref, halos[:2]),
    )
    for normal, prims, split, read, _, flux, _ in plans:
        split_own(normal, prims, split, read)
        differences(3, 10, split)
        faces_across(normal, 3, 6, prims, split, flux)
    for normal, prims, split, _, read, flux, copies in plans:
        for copy in copies:
            copy.wait()
        cells_halo(normal, prims, split, read)
        differences(0, 3, split)
        differences(10, 13, split)
        faces_across(normal, 0, 3, prims, split, flux)
        faces_across(normal, 6, 9, prims, split, flux)

    def y_rate(y, _):
        for r in range(NVAR):
            acc_ref[pl.ds(r * block + y, 8, stride=8), :] = fy_ref[r, y + 1] - fy_ref[r, y]
        return 0

    lax.fori_loop(0, 8, y_rate, 0)

    scale = (-COURANT / 6.0) / (alphas[0] + alphas[1] + alphas[2])
    near = jnp.where(lane < 2, lane + 3, lane - lanes + 13)
    patched = (lane < 2) | (lane > lanes - 4)

    def finish(x, _):
        first = jnp.clip(width * x + near, 0, lanes - 1)
        below = jnp.full(tile, width * x + 2, jnp.int32)
        for r in range(NVAR):
            edges = fz_ref[r, 8]
            upper = jnp.where(patched, gather(edges, first), fz_ref[r, x])
            lower = jnp.where(lane == 0, gather(edges, below), roll(upper, 1))
            rows = pl.ds(pl.multiple_of(r * block + x * 8, 8), 8)
            rate = (upper - lower) + (fx_ref[r, x + 1] - fx_ref[r, x]) + acc_ref[rows, :]
            out_ref[rows, :] = scale * rate
        return 0

    lax.fori_loop(0, 8, finish, 0)


def shards(preserved_vector, nasa_table, gas_constant, species_index, face_kind):
    _, nx, ny, lanes = preserved_vector.shape
    size_x, size_y = lax.axis_size("gx"), lax.axis_size("gy")
    flat = preserved_vector.reshape(NVAR * nx * ny, lanes)
    smem = pl.BlockSpec(memory_space=pltpu.SMEM)
    anywhere = pl.BlockSpec(memory_space=pl.ANY)
    dma = pltpu.SemaphoreType.DMA

    def buffer(*shape):
        return pltpu.VMEM(shape + (8, lanes), jnp.float32)

    out = pl.pallas_call(
        functools.partial(fused, size_x, size_y),
        out_shape=jax.ShapeDtypeStruct(flat.shape, jnp.float32),
        in_specs=[smem] * 4 + [anywhere] * 3,
        out_specs=pl.BlockSpec(memory_space=pltpu.VMEM),
        scratch_shapes=[
            pltpu.VMEM(flat.shape, jnp.float32),
            buffer(2, NVAR, 3),
            pltpu.VMEM((2, NVAR, nx, 3, 1, lanes), jnp.float32),
            buffer(),
            buffer(),
            buffer(size_y),
            buffer(size_x),
            buffer(TABLE),
            buffer(PRIMS + 1, 15),
            buffer(PRIMS + 1, 15),
            buffer(NVAR + 1, 15),
            buffer(NVAR + 1, 15),
            buffer(NVAR + 1, 15),
            buffer(NVAR + 1, 15),
            buffer(NVAR, 9),
            buffer(NVAR, 9),
            pltpu.VMEM(flat.shape, jnp.float32),
            buffer(NVAR),
            buffer(NVAR, 9),
            *[buffer(NVAR + 1, 15) for _ in range(4)],
            dma(()),
            dma((size_x + size_y,)),
            dma((size_y,)),
            dma((size_x,)),
            dma((4,)),
            dma((4,)),
        ],
        compiler_params=pltpu.CompilerParams(collective_id=0, has_side_effects=True),
        name="increment",
    )(
        nasa_table.T, gas_constant, species_index, face_kind.reshape(2), flat,
        preserved_vector, preserved_vector.reshape(NVAR, nx, ny, 1, lanes),
    )
    return out.reshape(preserved_vector.shape)


def solution(mesh):
    return jax.shard_map(
        shards,
        mesh=mesh,
        in_specs=(P(None, "gx", "gy", None), P(), P(), P(), P("gx", "gy", None)),
        out_specs=P(None, "gx", "gy", None),
        check_vma=False,
    )
```

profile of v0, /device:TPU:0, one launch (start us, length us, event | category | flops | bytes accessed | tf_op | source)
XLA Modules:
  0.0 30.9 jit_solution(9103034668623389379)
XLA Ops:
  0.0 29.1 %increment.1 = f32[896,128]{1,0:T(8,128)} custom-call(f32[6,32]{1,0:T(8,128)} %bitcast.8, f32[32]{0:T(128)} %gas_ref.1, s32[9]{0:T(128)} %index_ref.1, s32[2]{0:T(128)} %bitcast.9, f32[896,128]{1,0:T(8,128)} %bitcast.5, f32[14,8,8,128]{3,2,1,0:T(8,128)} %planes_ref.1, f32[14,8,8,1,128]{4,3,2,1,0:T(1,128)} %bitcast.6), custom_call_target="tpu_custom_call" | custom-call | tf_op jit(solution)/shard_map/increment/pallas_call | solution.py:491
  29.1 1.8 %copy.7 = f32[14,8,8,128]{3,2,1,0:T(8,128)} copy(f32[14,8,8,128]{3,2,1,0:T(8,128)} %bitcast.7) | data formatting | bytes 917504
where the time goes:
time: 31.1 us; the launch traced here: 30.9 us
  Pallas kernels  29.1 us (94%)
  local copies, waits for them, and re-layouts  1.82 us (6%)
    pallas_call x1, Pallas kernels, shards(): pl.pallas_call(functools.partial(fused, size_x, size_y), out_shape=jax.Sh...  29.1 us
    unnamed x1, local copies, waits for them, and re-layouts  1.82 us

commit v1 on v0

--- a/solution.py
+++ b/solution.py
@@ -198,49 +198,41 @@
 
 def fused(
     size_x, size_y,
-    nasa_ref, gas_ref, index_ref, kind_ref, flat_ref, planes_ref, source_ref, out_ref,
-    x_ref, hx_ref, hy_ref, mine_ref, line_ref, slots_y, slots_x,
+    nasa_hbm, gas_hbm, index_hbm, kind_hbm, flat_ref, planes_ref, source_ref, out_ref,
+    nasa_ref, gas_ref, index_ref, kind_ref,
+    x_ref, hx_ref, hy_ref, mine_ref, slots_ref,
     table_ref, prim_ref, turn_ref, up_ref, down_ref, dup_ref, ddown_ref,
     fx_ref, fz_ref, acc_ref, edge_ref, fy_ref, s0_ref, s1_ref, s2_ref, s3_ref,
-    load_sem, small_send, recv_y, recv_x, big_send, big_recv,
+    load_sem, param_sem, small_send, small_recv, big_send, big_recv,
 ):
     load = pltpu.make_async_copy(flat_ref, x_ref, load_sem)
     load.start()
+    params = [
+        pltpu.make_async_copy(source, target, param_sem.at[n])
+        for n, (source, target) in enumerate(
+            (
+                (nasa_hbm, nasa_ref),
+                (gas_hbm, gas_ref),
+                (index_hbm, index_ref),
+                (kind_hbm, kind_ref),
+            )
+        )
+    ]
+    for copy in params:
+        copy.start()
     gx, gy = lax.axis_index("gx"), lax.axis_index("gy")
     nx, ny = planes_ref.shape[1], planes_ref.shape[2]
 
-    def along_x(offset):
-        return (lax.rem(gx + offset, size_x), gy)
-
-    def along_y(offset):
-        return (gx, lax.rem(gy + offset, size_y))
-
+    def there(ox, oy):
+        return (lax.rem(gx + ox, size_x), lax.rem(gy + oy, size_y))
+
+    others = [(ox, oy) for ox in range(size_x) for oy in range(size_y) if ox or oy]
     barrier = pltpu.get_barrier_semaphore()
-    for n, along in ((size_x, along_x), (size_y, along_y)):
-        for offset in range(1, n):
-            pl.semaphore_signal(barrier, inc=1, device_id=along(offset), device_id_type=MESH)
+    for ox, oy in others:
+        pl.semaphore_signal(barrier, inc=1, device_id=there(ox, oy), device_id_type=MESH)
+    for copy in params:
+        copy.wait()
     fill_table(nasa_ref, gas_ref, index_ref, table_ref)
-    pl.semaphore_wait(barrier, size_x + size_y - 2)
-
-    halos = []
-    for n, (source, target, device) in enumerate(
-        (
-            (planes_ref.at[:, pl.ds(nx - 3, 3)], hx_ref.at[0], along_x(1)),
-            (planes_ref.at[:, pl.ds(0, 3)], hx_ref.at[1], along_x(size_x - 1)),
-            (source_ref.at[:, :, pl.ds(ny - 3, 3)], hy_ref.at[0], along_y(1)),
-            (source_ref.at[:, :, pl.ds(0, 3)], hy_ref.at[1], along_y(size_y - 1)),
-        )
-    ):
-        copy = pltpu.make_async_remote_copy(
-            src_ref=source,
-            dst_ref=target,
-            send_sem=big_send.at[n],
-            recv_sem=big_recv.at[n],
-            device_id=device,
-            device_id_type=MESH,
-        )
-        copy.start()
-        halos.append(copy)
     load.wait()
 
     lanes = x_ref.shape[1]
@@ -394,40 +386,59 @@
     zero = jnp.zeros(tile, jnp.float32)
     best = lax.fori_loop(0, 8, x_prims, (zero, zero, zero))
     best = [jnp.max(b, axis=(0, 1), keepdims=True) for b in best]
-    row = lax.broadcasted_iota(jnp.int32, tile, 0)
-    value = jnp.where(row == 0, best[0], jnp.where(row == 1, best[1], best[2]))
-
-    def fill_turned():
-        lax.fori_loop(0, 8, y_prims, 0)
-
-    def fill_edge():
-        for r in range(NVAR):
-            edge_ref[r] = zero
-        lax.fori_loop(0, 8, z_edge, 0)
-        fill_cells([edge_ref[r] for r in range(NVAR)], 14, table_ref, prim_ref)
-
-    for n, along, held, slots, recv, base, meanwhile in (
-        (size_y, along_y, mine_ref, slots_y, recv_y, 0, fill_edge),
-        (size_x, along_x, line_ref, slots_x, recv_x, size_y, fill_turned),
+    column = lax.broadcasted_iota(jnp.int32, (1, lanes), 1)
+    mine_ref[...] = jnp.where(column == 0, best[0], jnp.where(column == 1, best[1], best[2]))
+    pl.semaphore_wait(barrier, len(others))
+
+    peers = []
+    for n, (ox, oy) in enumerate(others):
+        copy = pltpu.make_async_remote_copy(
+            src_ref=mine_ref,
+            dst_ref=slots_ref.at[n],
+            send_sem=small_send.at[n],
+            recv_sem=small_recv.at[n],
+            device_id=there(ox, oy),
+            device_id_type=MESH,
+        )
+        copy.start()
+        peers.append(copy)
+    halos = []
+    for n, (origin, target, device) in enumerate(
+        (
+            (planes_ref.at[:, pl.ds(nx - 3, 3)], hx_ref.at[0], there(1, 0)),
+            (planes_ref.at[:, pl.ds(0, 3)], hx_ref.at[1], there(size_x - 1, 0)),
+            (source_ref.at[:, :, pl.ds(ny - 3, 3)], hy_ref.at[0], there(0, 1)),
+            (source_ref.at[:, :, pl.ds(0, 3)], hy_ref.at[1], there(0, size_y - 1)),
+        )
     ):
-        held[...] = value
-        copies = []
-        for offset in range(1, n):
-            copy = pltpu.make_async_remote_copy(
-                src_ref=held,
-                dst_ref=slots.at[offset],
-                send_sem=small_send.at[base + offset],
-                recv_sem=recv.at[offset],
-                device_id=along(offset),
-                device_id_type=MESH,
-            )
-            copy.start()
-            copies.append(copy)
-        meanwhile()
-        for offset, copy in enumerate(copies, 1):
-            copy.wait()
-            value = jnp.maximum(value, slots[offset])
-    alphas = [jnp.broadcast_to(value[d : d + 1], tile) for d in range(3)]
+        copy = pltpu.make_async_remote_copy(
+            src_ref=origin,
+            dst_ref=target,
+            send_sem=big_send.at[n],
+            recv_sem=big_recv.at[n],
+            device_id=device,
+            device_id_type=MESH,
+        )
+        copy.start()
+        halos.append(copy)
+
+    for r in range(NVAR):
+        edge_ref[r] = zero
+    lax.fori_loop(0, 8, z_edge, 0)
+    fill_cells([edge_ref[r] for r in range(NVAR)], 14, table_ref, prim_ref)
+    lax.fori_loop(0, 8, y_prims, 0)
+
+    for copy in peers:
+        copy.wait()
+    value = mine_ref[...]
+    for n in range(len(others)):
+        value = jnp.maximum(value, slots_ref[n])
+    alphas = [
+        jnp.broadcast_to(
+            jnp.max(jnp.where(column == d, value, 0.0), axis=1, keepdims=True), tile
+        )
+        for d in range(3)
+    ]
 
     z_split([edge_ref[r] for r in range(NVAR)], 14)
     lax.fori_loop(0, 8, z_own, 0)
@@ -481,8 +492,7 @@
     _, nx, ny, lanes = preserved_vector.shape
     size_x, size_y = lax.axis_size("gx"), lax.axis_size("gy")
     flat = preserved_vector.reshape(NVAR * nx * ny, lanes)
-    smem = pl.BlockSpec(memory_space=pltpu.SMEM)
-    anywhere = pl.BlockSpec(memory_space=pl.ANY)
+    hbm = pl.BlockSpec(memory_space=pltpu.HBM)
     dma = pltpu.SemaphoreType.DMA
 
     def buffer(*shape):
@@ -491,16 +501,18 @@
     out = pl.pallas_call(
         functools.partial(fused, size_x, size_y),
         out_shape=jax.ShapeDtypeStruct(flat.shape, jnp.float32),
-        in_specs=[smem] * 4 + [anywhere] * 3,
+        in_specs=[hbm] * 7,
         out_specs=pl.BlockSpec(memory_space=pltpu.VMEM),
         scratch_shapes=[
+            pltpu.SMEM(nasa_table.T.shape, jnp.float32),
+            pltpu.SMEM(gas_constant.shape, jnp.float32),
+            pltpu.SMEM(species_index.shape, jnp.int32),
+            pltpu.SMEM((2,), jnp.int32),
             pltpu.VMEM(flat.shape, jnp.float32),
             buffer(2, NVAR, 3),
             pltpu.VMEM((2, NVAR, nx, 3, 1, lanes), jnp.float32),
-            buffer(),
-            buffer(),
-            buffer(size_y),
-            buffer(size_x),
+            pltpu.VMEM((1, lanes), jnp.float32),
+            pltpu.VMEM((size_x * size_y - 1, 1, lanes), jnp.float32),
             buffer(TABLE),
             buffer(PRIMS + 1, 15),
             buffer(PRIMS + 1, 15),
@@ -515,13 +527,15 @@
             buffer(NVAR, 9),
             *[buffer(NVAR + 1, 15) for _ in range(4)],
             dma(()),
-            dma((size_x + size_y,)),
-            dma((size_y,)),
-            dma((size_x,)),
+            dma((4,)),
+            dma((size_x * size_y - 1,)),
+            dma((size_x * size_y - 1,)),
             dma((4,)),
             dma((4,)),
         ],
-        compiler_params=pltpu.CompilerParams(collective_id=0, has_side_effects=True),
+        compiler_params=pltpu.CompilerParams(
+            collective_id=0, has_side_effects=True, vmem_limit_bytes=20 * 1024 * 1024
+        ),
         name="increment",
     )(
         nasa_table.T, gas_constant, species_index, face_kind.reshape(2), flat,

time: 31.1 us -> 27.1 us (0.87)
  the two profiles are of different devices: /device:TPU:0 before, /device:TPU:3 now
where the time goes in v1:
time: 27.1 us; the launch traced here: 27 us
  Pallas kernels  24.5 us (90%)
  local copies, waits for them, and re-layouts  2.48 us (9%)
    pallas_call x1, Pallas kernels, shards(): pl.pallas_call(functools.partial(fused, size_x, size_y), out_shape=jax.Sh...  24.5 us
    unnamed x11, local copies, waits for them, and re-layouts  2.48 us

profile of v1, /device:TPU:3, one launch (start us, length us, event | category | flops | bytes accessed | tf_op | source)
XLA Modules:
  0.0 27.0 jit_solution(7083149657242919348)
XLA Ops:
  0.0 0.0 copy-start.1
  0.0 0.0 copy-start.2
  0.0 0.0 copy-start.3
  0.0 0.0 copy-start.4
  0.0 0.7 %copy-done.1 = f32[32,6]{0,1:T(8,128)S(1)} copy-done((f32[32,6]{0,1:T(8,128)S(1)}, f32[32,6]{0,1:T(8,128)}, u32[]{:S(2)}) %copy-start.1) | copy-done | bytes 792
  0.7 0.0 copy-done.2
  0.7 0.0 copy-done.3
  0.7 0.0 copy-done.4
  0.7 0.0 copy-start
  0.7 1.0 %copy-done = f32[14,8,8,128]{3,2,1,0:T(8,128)S(1)} copy-done((f32[14,8,8,128]{3,2,1,0:T(8,128)S(1)}, f32[14,8,8,128]{3,2,1,0:T(8,128)}, u32[]{:S(2)}) %copy-start) | copy-done | bytes 458776
  1.7 24.5 %increment.1 = f32[896,128]{1,0:T(8,128)S(1)} custom-call(f32[6,32]{1,0:T(8,128)S(1)} %bitcast.8, f32[32]{0:T(128)S(1)} %copy-done.2, s32[9]{0:T(128)S(1)} %copy-done.3, s32[2]{0:T(128)S(1)} %bitcast.9, f32[896,128]{1,0:T(8,128)S(1)} %bitcast.5, f32[14,8,8,128]{3,2,1,0:T(8,128)S(1)} %copy-done, f32[14,8,8,1,128]{4,3,2,1,0:T(1,128)S(1)} %bitcast.6), custom_call_target="tpu_custom_call" | custom-call | tf_op jit(solution)/shard_map/increment/pallas_call | solution.py:501
  26.2 0.8 %copy.7 = f32[14,8,8,128]{3,2,1,0:T(8,128)} copy(f32[14,8,8,128]{3,2,1,0:T(8,128)S(1)} %bitcast.7) | data formatting | bytes 917504
Async XLA Ops:
  0.0 0.7 %copy-start.1 = (f32[32,6]{0,1:T(8,128)S(1)}, f32[32,6]{0,1:T(8,128)}, u32[]{:S(2)}) copy-start(f32[32,6]{0,1:T(8,128)} %param.6) | copy-start | bytes 2308
  0.0 0.7 %copy-start.2 = (f32[32]{0:T(128)S(1)}, f32[32]{0:T(128)}, u32[]{:S(2)}) copy-start(f32[32]{0:T(128)} %gas_hbm.1) | copy-start | bytes 388
  0.0 0.7 %copy-start.3 = (s32[9]{0:T(128)S(1)}, s32[9]{0:T(128)}, u32[]{:S(2)}) copy-start(s32[9]{0:T(128)} %index_hbm.1) | copy-start | bytes 112
  0.0 0.7 %copy-start.4 = (s32[1,1,2]{2,1,0:T(1,128)S(1)}, s32[1,1,2]{2,1,0:T(1,128)}, u32[]{:S(2)}) copy-start(s32[1,1,2]{2,1,0:T(1,128)} %param.9) | copy-start | bytes 28
  0.7 1.0 %copy-start = (f32[14,8,8,128]{3,2,1,0:T(8,128)S(1)}, f32[14,8,8,128]{3,2,1,0:T(8,128)}, u32[]{:S(2)}) copy-start(f32[14,8,8,128]{3,2,1,0:T(8,128)} %planes_ref.1) | copy-start | bytes 1376260

commit v2 on v1

v2 whole, which is shorter than its diff:
```python
import functools

import jax
import jax.numpy as jnp
from jax import lax
from jax.experimental import pallas as pl
from jax.experimental.pallas import tpu as pltpu
from jax.sharding import PartitionSpec as P

NS = 9
NVAR = 14
EPSILON = 1e-06
COURANT = 0.8
TOTAL = NVAR
PRIMS = 24
VEL, PASSIVE, GAMMA, SOUND, SLOPES = 9, 12, 13, 14, 15
TABLE = 7 * NS
ORDER = ((0, 1, 2), (1, 0, 2), (2, 0, 1))
PARTS = 7
ROW = 2 * PARTS + 2
STEEP, ENTHALPY, SQUARE = 14, 23, 24
COEFS = 25
FACES = 9
MESH = pl.DeviceIdType.MESH


def fill_table(nasa_ref, gas_ref, index_ref, table_ref):
    for i in range(NS):
        row = index_ref[i]
        gas = gas_ref[row]
        values = [
            gas,
            gas * nasa_ref[5, row],
            gas * (nasa_ref[0, row] - 1.0),
            gas * nasa_ref[1, row] * (1.0 / 2.0),
            gas * nasa_ref[2, row] * (1.0 / 3.0),
            gas * nasa_ref[3, row] * (1.0 / 4.0),
            gas * nasa_ref[4, row] * (1.0 / 5.0),
        ]
        for n, value in enumerate(values):
            table_ref[n * NS + i] = jnp.full(table_ref.shape[1:], value, jnp.float32)


def tree(terms):
    terms = list(terms)
    while len(terms) > 1:
        terms = [a + b for a, b in zip(terms[::2], terms[1::2])] + (
            [terms[-1]] if len(terms) % 2 else []
        )
    return terms[0]


def thermo(u, table_ref):
    rho = tree(u[:NS])
    inverse = 1.0 / rho
    vel = [m * inverse for m in u[NS : NS + 3]]
    inner = u[NS + 3] - 0.5 * tree([v * m for v, m in zip(vel, u[NS : NS + 3])])
    mix = [tree([u[i] * table_ref[n * NS + i] for i in range(NS)]) for n in range(7)]
    gas, m6, m1, m2, m3, m4, m5 = mix
    c2, c3, c4, c5 = 2.0 * m2, 3.0 * m3, 4.0 * m4, 5.0 * m5
    temp = 1.0 - (tree([m6, m1, m2, m3, m4, m5]) - inner) / tree([m1, c2, c3, c4, c5])

    def heat(t):
        return m1 + t * (c2 + t * (c3 + t * (c4 + t * c5)))

    energy = m6 + temp * (m1 + temp * (m2 + temp * (m3 + temp * (m4 + temp * m5))))
    temp = temp - (energy - inner) / heat(temp)
    pressure = temp * gas
    gamma = gas / heat(temp)
    sound = jnp.sqrt((1.0 + gamma) * pressure * inverse)
    return inverse, vel, temp, pressure, gamma, sound


def slopes_of(temp, gamma, square, table_ref):
    kinetic = 0.5 * gamma * square
    result = []
    for i in range(NS):
        k = [table_ref[n * NS + i] for n in range(7)]
        e = k[1] + temp * (k[2] + temp * (k[3] + temp * (k[4] + temp * (k[5] + temp * k[6]))))
        result.append(k[0] * temp - gamma * e + kinetic)
    return result


def reciprocal(x):
    return pl.reciprocal(x, approx=True)


def correction(d1, d2, e0, e1, e2):
    h1, h2 = 0.75 * d1, 0.75 * d2
    near, far = h1 * d1 + 0.75 * EPSILON, h2 * d2 + 0.75 * EPSILON
    r0 = reciprocal(e0 * (e0 + h1) + near)
    r1 = reciprocal(e1 * (e1 + h1) + near)
    r2 = reciprocal(e2 * (e2 - h2) + far)
    a = r0 * r0 * (1.0 / 3.0)
    b = r1 * r1
    c = r2 * r2
    g0, g2 = e0 - e1, e1 - e2
    return (a * (g0 + g0) + c * g2) * reciprocal(a + c + (b + b))


def fused(
    size_x, size_y,
    nasa_hbm, gas_hbm, index_hbm, kind_hbm, flat_ref, planes_ref, out_ref,
    nasa_ref, gas_ref, index_ref, kind_ref,
    x_ref, z_ref, acc_ref, back_ref, hx_ref, sy_ref, hy_ref, mine_ref, slots_ref,
    table_ref, cache_ref, prim_ref, f_ref, u_ref, df_ref, du_ref,
    part_ref, coef_ref, alpha_ref, flux_ref,
    load_sem, param_sem, small_send, small_recv, big_send, big_recv,
):
    load = pltpu.make_async_copy(flat_ref, x_ref, load_sem)
    load.start()
    params = [
        pltpu.make_async_copy(origin, target, param_sem.at[n])
        for n, (origin, target) in enumerate(
            (
                (nasa_hbm, nasa_ref),
                (gas_hbm, gas_ref),
                (index_hbm, index_ref),
                (kind_hbm, kind_ref),
            )
        )
    ]
    for copy in params:
        copy.start()
    gx, gy = lax.axis_index("gx"), lax.axis_index("gy")
    nx, ny = planes_ref.shape[1], planes_ref.shape[2]
    lanes = x_ref.shape[1]
    tile = (8, lanes)
    block = nx * ny

    def there(ox, oy):
        return (lax.rem(gx + ox, size_x), lax.rem(gy + oy, size_y))

    others = [(ox, oy) for ox in range(size_x) for oy in range(size_y) if ox or oy]
    barrier = pltpu.get_barrier_semaphore()
    for ox, oy in others:
        pl.semaphore_signal(barrier, inc=1, device_id=there(ox, oy), device_id_type=MESH)
    for copy in params:
        copy.wait()
    fill_table(nasa_ref, gas_ref, index_ref, table_ref)
    load.wait()

    def own(r, x):
        return x_ref[pl.ds(pl.multiple_of(r * block + x * 8, 8), 8), :]

    def turned(r, y):
        return x_ref[pl.ds(r * block + y, 8, stride=8), :]

    def upright(r, t):
        return z_ref[pl.ds(r * block + t, 8, stride=8), :]

    def flow(d, p, u, vel, pressure):
        order = ORDER[d]
        speed = vel[order[0]]
        half, push = 0.5 * speed, 0.5 * pressure
        rows = list(range(NS)) + [NS + n for n in order] + [NS + 3, NS + 4]
        for k, r in enumerate(rows):
            value = u[r] * half
            if k == NS:
                value = value + push
            if k == NS + 3:
                value = value + push * speed
            f_ref[d, p, k] = value
            u_ref[d, p, k] = 0.5 * u[r]
        rho = tree(u[:NS])
        f_ref[d, p, TOTAL] = rho * half
        u_ref[d, p, TOTAL] = 0.5 * rho

    def cells(d, p, u, state):
        inverse, vel, temp, pressure, gamma, sound = state
        flow(d, p, u, vel, pressure)
        q = p - 2
        for k in range(NS):
            prim_ref[d, q, k] = u[k] * inverse
        for k in range(3):
            prim_ref[d, q, VEL + k] = vel[ORDER[d][k]]
        prim_ref[d, q, PASSIVE] = u[NS + 4] * inverse
        prim_ref[d, q, GAMMA] = gamma
        prim_ref[d, q, SOUND] = sound
        square = tree([v * v for v in vel])
        for k, value in enumerate(slopes_of(temp, gamma, square, table_ref)):
            prim_ref[d, q, SLOPES + k] = value

    def own_cells(d, read):
        def step(n, _):
            u = [read(r, n) for r in range(NVAR)]
            cells(d, n + 3, u, thermo(u, table_ref))
            return 0

        lax.fori_loop(0, 8, step, 0)

    def halo_cells(d, read):
        for side, k, p in ((0, 2, 2), (1, 0, 11)):
            u = [read(side, r, k) for r in range(NVAR)]
            cells(d, p, u, thermo(u, table_ref))

        def step(k, _):
            for side, base in ((0, 0), (1, 11)):
                u = [read(side, r, k + side) for r in range(NVAR)]
                _, vel, _, pressure, _, _ = thermo(u, table_ref)
                flow(d, k + side + base, u, vel, pressure)
            return 0

        lax.fori_loop(0, 2, step, 0)

    def differences(d, first, last):
        def step(p, _):
            for k in range(NVAR + 1):
                df_ref[d, p, k] = f_ref[d, p + 1, k] - f_ref[d, p, k]
                du_ref[d, p, k] = u_ref[d, p + 1, k] - u_ref[d, p, k]
            return 0

        lax.fori_loop(first, last, step, 0)

    def project(d, first, last, start):
        def step(i, _):
            g = i + (start - first)

            def mean(q):
                return 0.5 * (prim_ref[d, i, q] + prim_ref[d, i + 1, q])

            y = [mean(k) for k in range(NS)]
            vel = [mean(VEL + k) for k in range(3)]
            phi = [mean(SLOPES + k) for k in range(NS)]
            z, gamma, sound = mean(PASSIVE), mean(GAMMA), mean(SOUND)
            inv = 1.0 / sound
            inv2, half_inv = inv * inv, 0.5 * inv
            steep = 1.0 / gamma
            for k in range(NS):
                coef_ref[g, k] = y[k]
                coef_ref[g, STEEP + k] = phi[k] * steep
            for k in range(3):
                coef_ref[g, VEL + k] = vel[k]
            coef_ref[g, PASSIVE] = z
            coef_ref[g, GAMMA] = sound
            coef_ref[g, ENTHALPY] = (
                sound * sound - tree([a * b for a, b in zip(y, phi)])
            ) * steep
            coef_ref[g, SQUARE] = tree([v * v for v in vel])
            for half, ref in enumerate((df_ref, du_ref)):

                def keep(n, d5):
                    at = n * ROW + half * PARTS
                    for j in range(3):
                        part_ref[g, at + j] = d5[j + 1]
                    for j in range(4):
                        part_ref[g, at + 3 + j] = d5[j + 1] - d5[j]

                waves = [[] for _ in range(5)]
                for k in range(5):
                    s = ref[d, i + k, TOTAL]
                    m = [ref[d, i + k, NS + n] for n in range(3)]
                    dp = tree([phi[n] * ref[d, i + k, n] for n in range(NS)]) + gamma * (
                        ref[d, i + k, NS + 3] - tree([vel[n] * m[n] for n in range(3)])
                    )
                    scaled = dp * inv2
                    jump = (m[0] - vel[0] * s) * half_inv
                    middle = 0.5 * scaled
                    waves[0].append(scaled)
                    waves[1].append(middle - jump)
                    waves[2].append(m[1] - vel[1] * s)
                    waves[3].append(m[2] - vel[2] * s)
                    waves[4].append(middle + jump)
                for n in range(4):
                    keep(NS + n, waves[n + 1])
                for n, share in enumerate(y):
                    keep(n, [ref[d, i + k, n] - share * waves[0][k] for k in range(5)])
                keep(NS + 4, [ref[d, i + k, NS + 4] - z * waves[0][k] for k in range(5)])
            for n in range(NVAR):
                part_ref[g, n * ROW + 2 * PARTS] = 6.0 * (
                    f_ref[d, i + 2, n] + f_ref[d, i + 3, n]
                ) + (df_ref[d, i + 1, n] - df_ref[d, i + 3, n])
                centre = du_ref[d, i + 2, n]
                part_ref[g, n * ROW + 2 * PARTS + 1] = (du_ref[d, i + 1, n] - centre) + (
                    du_ref[d, i + 3, n] - centre
                )
            return 0

        lax.fori_loop(first, last, step, 0)

    def advance(first, last):
        def step(g, _):
            alpha = alpha_ref[g]

            def wave(n):
                f = [part_ref[g, n * ROW + j] for j in range(PARTS)]
                t = [alpha * part_ref[g, n * ROW + PARTS + j] for j in range(PARTS)]
                rising = correction(f[0] + t[0], f[1] + t[1], f[3] + t[3], f[4] + t[4], f[5] + t[5])
                falling = correction(f[2] - t[2], f[1] - t[1], t[6] - f[6], t[5] - f[5], t[4] - f[4])
                return rising - falling

            def linear(n):
                at = n * ROW + 2 * PARTS
                return part_ref[g, at] + alpha * part_ref[g, at + 1]

            slower, faster = wave(NS), wave(NS + 3)
            shears = [wave(NS + 1), wave(NS + 2)]
            acoustic = slower + faster
            total, weighted = None, None
            for n in range(NS):
                amp = wave(n)
                flux_ref[g, n] = linear(n) + coef_ref[g, n] * acoustic + amp
                steep = coef_ref[g, STEEP + n] * amp
                total = amp if n == 0 else total + amp
                weighted = steep if n == 0 else weighted + steep
            amp = wave(NS + 4)
            flux_ref[g, NS + 4] = linear(NS + 4) + coef_ref[g, PASSIVE] * acoustic + amp
            mass = acoustic + total
            swing = coef_ref[g, GAMMA] * (faster - slower)
            vel = [coef_ref[g, VEL + n] for n in range(3)]
            flux_ref[g, NS] = linear(NS) + vel[0] * mass + swing
            flux_ref[g, NS + 1] = linear(NS + 1) + vel[1] * mass + shears[0]
            flux_ref[g, NS + 2] = linear(NS + 2) + vel[2] * mass + shears[1]
            flux_ref[g, NS + 3] = (
                linear(NS + 3)
                + coef_ref[g, SQUARE] * mass
                + (coef_ref[g, ENTHALPY] * acoustic - weighted)
                + vel[0] * swing
                + vel[1] * shears[0]
                + vel[2] * shears[1]
            )
            return 0

        lax.fori_loop(first, last, step, 0)

    for side, first in ((0, ny - 3), (1, 0)):
        for k in range(3):
            for r in range(NVAR):
                sy_ref[side, k, r] = turned(r, first + k)

    def x_state(x, best):
        u = [own(r, x) for r in range(NVAR)]
        inverse, vel, temp, pressure, gamma, sound = thermo(u, table_ref)
        for k, value in enumerate([inverse, *vel, temp, pressure, gamma, sound]):
            cache_ref[x, k] = value
        return tuple(jnp.maximum(b, jnp.abs(v) + sound) for b, v in zip(best, vel))

    zero = jnp.zeros(tile, jnp.float32)
    best = lax.fori_loop(0, 8, x_state, (zero, zero, zero))
    best = [jnp.max(b, axis=(0, 1), keepdims=True) for b in best]
    column = lax.broadcasted_iota(jnp.int32, (1, lanes), 1)
    mine_ref[...] = jnp.where(column == 0, best[0], jnp.where(column == 1, best[1], best[2]))
    pl.semaphore_wait(barrier, len(others))

    peers = []
    for n, (ox, oy) in enumerate(others):
        copy = pltpu.make_async_remote_copy(
            src_ref=mine_ref,
            dst_ref=slots_ref.at[n],
            send_sem=small_send.at[n],
            recv_sem=small_recv.at[n],
            device_id=there(ox, oy),
            device_id_type=MESH,
        )
        copy.start()
        peers.append(copy)
    halos = []
    for n, (origin, target, device) in enumerate(
        (
            (planes_ref.at[:, pl.ds(nx - 3, 3)], hx_ref.at[0], there(1, 0)),
            (planes_ref.at[:, pl.ds(0, 3)], hx_ref.at[1], there(size_x - 1, 0)),
            (sy_ref.at[0], hy_ref.at[0], there(0, 1)),
            (sy_ref.at[1], hy_ref.at[1], there(0, size_y - 1)),
        )
    ):
        copy = pltpu.make_async_remote_copy(
            src_ref=origin,
            dst_ref=target,
            send_sem=big_send.at[n],
            recv_sem=big_recv.at[n],
            device_id=device,
            device_id_type=MESH,
        )
        copy.start()
        halos.append(copy)

    def x_cells(x, _):
        u = [own(r, x) for r in range(NVAR)]
        state = [cache_ref[x, k] for k in range(8)]
        cells(0, x + 3, u, (state[0], state[1:4], *state[4:]))
        return 0

    side_by_side = lax.broadcasted_iota(jnp.int32, (block, lanes), 1) < block

    def flip(a):
        b = jnp.concatenate([a, a], axis=0).T
        return jnp.where(side_by_side, b[:block], b[block:])

    for r in range(NVAR):
        z_ref[pl.ds(r * block, block), :] = flip(x_ref[pl.ds(r * block, block), :])
    lax.fori_loop(0, 8, x_cells, 0)
    own_cells(1, turned)
    own_cells(2, upright)

    lane = lax.broadcasted_iota(jnp.int32, tile, 1)
    row = lax.broadcasted_iota(jnp.int32, tile, 0)
    walls = kind_ref[0] == 1, kind_ref[1] == 1
    outside = (row == 0) & (lane < block), (row == 7) & (lane >= block)
    wrap = row == 0, row == 7

    def beyond(side, r, k):
        inner = upright(r, (7 - k) if side else (2 - k))
        edge = upright(r, 7 if side else 0)
        ghost = jnp.where(walls[side], -inner if r == NS + 2 else inner, edge)
        if side:
            along = pltpu.roll(upright(r, k), 7, 0)
        else:
            along = pltpu.roll(upright(r, 5 + k), 1, 0)
        across = pltpu.roll(along, block, 1)
        return jnp.where(outside[side], ghost, jnp.where(wrap[side], across, along))

    halo_cells(2, beyond)
    differences(0, 3, 10)
    differences(1, 3, 10)
    differences(2, 0, 13)
    project(2, 0, 9, 0)
    project(1, 3, 6, 9)
    project(0, 3, 6, 12)

    for copy in peers:
        copy.wait()
    value = mine_ref[...]
    for n in range(len(others)):
        value = jnp.maximum(value, slots_ref[n])
    alphas = [
        jnp.broadcast_to(
            jnp.max(jnp.where(column == d, value, 0.0), axis=1, keepdims=True), tile
        )
        for d in range(3)
    ]
    for g in range(3 * FACES):
        alpha_ref[g] = alphas[2 if g < 9 else 1 if g < 12 or 15 <= g < 21 else 0]

    advance(0, 15)
    for d, read, pair, start in (
        (1, lambda side, r, k: hy_ref[side, k, r], halos[2:], 15),
        (0, lambda side, r, k: hx_ref[side, r, k], halos[:2], 21),
    ):
        for copy in pair:
            copy.wait()
        halo_cells(d, read)
        differences(d, 0, 3)
        differences(d, 10, 13)
        project(d, 0, 3, start)
        project(d, 6, 9, start + 3)
        advance(start, start + 6)

    def slot(d, i):
        if d == 2:
            return i
        if 3 <= i < 6:
            return (9 if d else 12) + i - 3
        return (15 if d else 21) + (i if i < 3 else i - 3)

    scale = (-COURANT / 6.0) / (alphas[0] + alphas[1] + alphas[2])

    def rate(d, i, r):
        n = NS + ORDER[d].index(r - NS) if NS <= r < NS + 3 else r
        return flux_ref[slot(d, i + 1), n] - flux_ref[slot(d, i), n]

    for r in range(NVAR):
        for i in range(8):
            acc_ref[pl.ds(r * block + i, 8, stride=8), :] = rate(1, i, r)
            back_ref[pl.ds(r * block + i, 8, stride=8), :] = rate(2, i, r)
        back = flip(back_ref[pl.ds(r * block, block), :])
        for i in range(8):
            rows = pl.ds(r * block + i * 8, 8)
            out_ref[rows, :] = scale * (
                rate(0, i, r) + acc_ref[rows, :] + back[i * 8 : i * 8 + 8]
            )


def shards(preserved_vector, nasa_table, gas_constant, species_index, face_kind):
    _, nx, ny, lanes = preserved_vector.shape
    size_x, size_y = lax.axis_size("gx"), lax.axis_size("gy")
    others = size_x * size_y - 1
    flat = preserved_vector.reshape(NVAR * nx * ny, lanes)
    hbm = pl.BlockSpec(memory_space=pltpu.HBM)
    dma = pltpu.SemaphoreType.DMA

    def buffer(*shape):
        return pltpu.VMEM(shape + (8, lanes), jnp.float32)

    out = pl.pallas_call(
        functools.partial(fused, size_x, size_y),
        out_shape=pltpu.VMEM(flat.shape, jnp.float32),
        in_specs=[hbm] * 6,
        out_specs=pl.BlockSpec(memory_space=pltpu.VMEM),
        scratch_shapes=[
            pltpu.SMEM(nasa_table.T.shape, jnp.float32),
            pltpu.SMEM(gas_constant.shape, jnp.float32),
            pltpu.SMEM(species_index.shape, jnp.int32),
            pltpu.SMEM((2,), jnp.int32),
            *[pltpu.VMEM(flat.shape, jnp.float32) for _ in range(4)],
            buffer(2, NVAR, 3),
            buffer(2, 3, NVAR),
            buffer(2, 3, NVAR),
            pltpu.VMEM((1, lanes), jnp.float32),
            pltpu.VMEM((others, 1, lanes), jnp.float32),
            buffer(TABLE),
            buffer(8, 8),
            buffer(3, 10, PRIMS),
            buffer(3, 14, NVAR + 1),
            buffer(3, 14, NVAR + 1),
            buffer(3, 13, NVAR + 1),
            buffer(3, 13, NVAR + 1),
            buffer(3 * FACES, NVAR * ROW),
            buffer(3 * FACES, COEFS),
            buffer(3 * FACES),
            buffer(3 * FACES, NVAR),
            dma(()),
            dma((4,)),
            dma((others,)),
            dma((others,)),
            dma((4,)),
            dma((4,)),
        ],
        compiler_params=pltpu.CompilerParams(
            collective_id=0, has_side_effects=True, vmem_limit_bytes=60 * 1000 * 1000
        ),
        name="increment",
    )(
        nasa_table.T, gas_constant, species_index, face_kind.reshape(2), flat,
        preserved_vector,
    )
    return out.reshape(preserved_vector.shape)


def solution(mesh):
    return jax.shard_map(
        shards,
        mesh=mesh,
        in_specs=(P(None, "gx", "gy", None), P(), P(), P(), P("gx", "gy", None)),
        out_specs=P(None, "gx", "gy", None),
        check_vma=False,
    )
```

time: 27.1 us -> 22.1 us (0.82)
  the two profiles are of different devices: /device:TPU:3 before, /device:TPU:0 now
where the time goes in v2:
time: 22.1 us; the launch traced here: 21.9 us
  Pallas kernels  21.2 us (96%)
  local copies, waits for them, and re-layouts  0.77 us (3%)
    pallas_call x1, Pallas kernels, shards(): pl.pallas_call(functools.partial(fused, size_x, size_y), out_shape=pltpu....  21.2 us
    unnamed x1, local copies, waits for them, and re-layouts  0.77 us

profile of v2, /device:TPU:0, one launch (start us, length us, event | category | flops | bytes accessed | tf_op | source)
XLA Modules:
  0.0 21.9 jit_solution(11227914072055504456)
XLA Ops:
  0.0 21.2 %increment.1 = f32[896,128]{1,0:T(8,128)S(1)} custom-call(f32[6,32]{1,0:T(8,128)} %bitcast.6, f32[32]{0:T(128)} %gas_hbm.1, s32[9]{0:T(128)} %index_hbm.1, s32[2]{0:T(128)} %bitcast.7, f32[896,128]{1,0:T(8,128)} %bitcast.5, f32[14,8,8,128]{3,2,1,0:T(8,128)} %planes_ref.1), custom_call_target="tpu_custom_call" | custom-call | tf_op jit(solution)/shard_map/increment/pallas_call | solution.py:484
  21.2 0.8 %copy.7 = f32[14,8,8,128]{3,2,1,0:T(8,128)} copy(f32[14,8,8,128]{3,2,1,0:T(8,128)S(1)} %bitcast.4) | data formatting | bytes 917504

commit v3 on v2

--- a/solution.py
+++ b/solution.py
@@ -104,7 +104,7 @@
     nasa_ref, gas_ref, index_ref, kind_ref,
     x_ref, z_ref, acc_ref, back_ref, hx_ref, sy_ref, hy_ref, mine_ref, slots_ref,
     table_ref, cache_ref, prim_ref, f_ref, u_ref, df_ref, du_ref,
-    part_ref, coef_ref, alpha_ref, flux_ref,
+    part_ref, coef_ref, alpha_ref, flux_ref, up_ref, down_ref,
     load_sem, param_sem, small_send, small_recv, big_send, big_recv,
 ):
     load = pltpu.make_async_copy(flat_ref, x_ref, load_sem)
@@ -187,21 +187,17 @@
             cells(d, n + 3, u, thermo(u, table_ref))
             return 0
 
-        lax.fori_loop(0, 8, step, 0)
-
-    def halo_cells(d, read):
-        for side, k, p in ((0, 2, 2), (1, 0, 11)):
+        lax.fori_loop(0, 8, step, 0, unroll=2)
+
+    def halo_cells(d, side, read):
+        for k in range(3):
+            p = k + 11 * side
             u = [read(side, r, k) for r in range(NVAR)]
-            cells(d, p, u, thermo(u, table_ref))
-
-        def step(k, _):
-            for side, base in ((0, 0), (1, 11)):
-                u = [read(side, r, k + side) for r in range(NVAR)]
-                _, vel, _, pressure, _, _ = thermo(u, table_ref)
-                flow(d, k + side + base, u, vel, pressure)
-            return 0
-
-        lax.fori_loop(0, 2, step, 0)
+            state = thermo(u, table_ref)
+            if p in (2, 11):
+                cells(d, p, u, state)
+            else:
+                flow(d, p, u, state[1], state[3])
 
     def differences(d, first, last):
         def step(p, _):
@@ -212,17 +208,51 @@
 
         lax.fori_loop(first, last, step, 0)
 
+    def split_inner(d):
+        def step(p, _):
+            for k in range(NVAR + 1):
+                push = alphas[d] * du_ref[d, p, k]
+                up_ref[d, p, k] = df_ref[d, p, k] + push
+                down_ref[d, p, k] = df_ref[d, p, k] - push
+            return 0
+
+        lax.fori_loop(3, 10, step, 0)
+
+    def split_outer(d, first):
+        def step(p, _):
+            for k in range(NVAR + 1):
+                step_f = f_ref[d, p + 1, k] - f_ref[d, p, k]
+                push = alphas[d] * (u_ref[d, p + 1, k] - u_ref[d, p, k])
+                up_ref[d, p, k] = step_f + push
+                down_ref[d, p, k] = step_f - push
+            return 0
+
+        lax.fori_loop(first, first + 3, step, 0)
+
+    def means(d, i):
+        def mean(q):
+            return 0.5 * (prim_ref[d, i, q] + prim_ref[d, i + 1, q])
+
+        y = [mean(k) for k in range(NS)]
+        vel = [mean(VEL + k) for k in range(3)]
+        phi = [mean(SLOPES + k) for k in range(NS)]
+        return y, vel, phi, mean(PASSIVE), mean(GAMMA), mean(SOUND)
+
+    def waves_of(get, vel, phi, gamma, inv2, half_inv):
+        s = get(TOTAL)
+        m = [get(NS + n) for n in range(3)]
+        dp = tree([phi[n] * get(n) for n in range(NS)]) + gamma * (
+            get(NS + 3) - tree([vel[n] * m[n] for n in range(3)])
+        )
+        scaled = dp * inv2
+        jump = (m[0] - vel[0] * s) * half_inv
+        middle = 0.5 * scaled
+        return scaled, middle - jump, m[1] - vel[1] * s, m[2] - vel[2] * s, middle + jump
+
     def project(d, first, last, start):
         def step(i, _):
             g = i + (start - first)
-
-            def mean(q):
-                return 0.5 * (prim_ref[d, i, q] + prim_ref[d, i + 1, q])
-
-            y = [mean(k) for k in range(NS)]
-            vel = [mean(VEL + k) for k in range(3)]
-            phi = [mean(SLOPES + k) for k in range(NS)]
-            z, gamma, sound = mean(PASSIVE), mean(GAMMA), mean(SOUND)
+            y, vel, phi, z, gamma, sound = means(d, i)
             inv = 1.0 / sound
             inv2, half_inv = inv * inv, 0.5 * inv
             steep = 1.0 / gamma
@@ -246,26 +276,15 @@
                     for j in range(4):
                         part_ref[g, at + 3 + j] = d5[j + 1] - d5[j]
 
-                waves = [[] for _ in range(5)]
-                for k in range(5):
-                    s = ref[d, i + k, TOTAL]
-                    m = [ref[d, i + k, NS + n] for n in range(3)]
-                    dp = tree([phi[n] * ref[d, i + k, n] for n in range(NS)]) + gamma * (
-                        ref[d, i + k, NS + 3] - tree([vel[n] * m[n] for n in range(3)])
-                    )
-                    scaled = dp * inv2
-                    jump = (m[0] - vel[0] * s) * half_inv
-                    middle = 0.5 * scaled
-                    waves[0].append(scaled)
-                    waves[1].append(middle - jump)
-                    waves[2].append(m[1] - vel[1] * s)
-                    waves[3].append(m[2] - vel[2] * s)
-                    waves[4].append(middle + jump)
+                waves = [
+                    waves_of(lambda n: ref[d, i + k, n], vel, phi, gamma, inv2, half_inv)
+                    for k in range(5)
+                ]
                 for n in range(4):
-                    keep(NS + n, waves[n + 1])
+                    keep(NS + n, [w[n + 1] for w in waves])
                 for n, share in enumerate(y):
-                    keep(n, [ref[d, i + k, n] - share * waves[0][k] for k in range(5)])
-                keep(NS + 4, [ref[d, i + k, NS + 4] - z * waves[0][k] for k in range(5)])
+                    keep(n, [ref[d, i + k, n] - share * waves[k][0] for k in range(5)])
+                keep(NS + 4, [ref[d, i + k, NS + 4] - z * waves[k][0] for k in range(5)])
             for n in range(NVAR):
                 part_ref[g, n * ROW + 2 * PARTS] = 6.0 * (
                     f_ref[d, i + 2, n] + f_ref[d, i + 3, n]
@@ -323,6 +342,90 @@
 
         lax.fori_loop(first, last, step, 0)
 
+    side_by_side = lax.broadcasted_iota(jnp.int32, (block, lanes), 1) < block
+
+    def flip(a):
+        b = jnp.concatenate([a, a], axis=0).T
+        return jnp.where(side_by_side, b[:block], b[block:])
+
+    def turn_back(r):
+        rows = pl.ds(pl.multiple_of(r * block, block), block)
+        back_ref[rows, :] = flip(back_ref[rows, :])
+
+    def direct(d, first, last, start):
+        def step(i, _):
+            g = i + (start - first)
+            y, vel, phi, z, gamma, sound = means(d, i)
+            inv = 1.0 / sound
+            inv2, half_inv = inv * inv, 0.5 * inv
+
+            def rising(n, k):
+                return up_ref[d, i + k, n]
+
+            def falling(n, k):
+                return down_ref[d, i + 4 - k, n]
+
+            sides = [
+                [
+                    waves_of(lambda n: get(n, k), vel, phi, gamma, inv2, half_inv)
+                    for k in range(4)
+                ]
+                for get in (rising, falling)
+            ]
+
+            def both(up, down):
+                pair = [
+                    correction(v[1], v[2], v[1] - v[0], v[2] - v[1], v[3] - v[2])
+                    for v in (up, down)
+                ]
+                return pair[0] - pair[1]
+
+            def wave(n):
+                return both(*[[w[n] for w in side] for side in sides])
+
+            def carried(n, share):
+                return both(
+                    [rising(n, k) - share * sides[0][k][0] for k in range(4)],
+                    [falling(n, k) - share * sides[1][k][0] for k in range(4)],
+                )
+
+            def linear(n):
+                ahead = up_ref[d, i + 2, n] - down_ref[d, i + 2, n]
+                return 6.0 * (f_ref[d, i + 2, n] + f_ref[d, i + 3, n]) + (
+                    (up_ref[d, i + 1, n] - down_ref[d, i + 3, n]) - ahead
+                )
+
+            slower, faster = wave(1), wave(4)
+            shears = [wave(2), wave(3)]
+            acoustic = slower + faster
+            total, weighted = None, None
+            for n in range(NS):
+                amp = carried(n, y[n])
+                flux_ref[g, n] = linear(n) + y[n] * acoustic + amp
+                term = phi[n] * amp
+                total = amp if n == 0 else total + amp
+                weighted = term if n == 0 else weighted + term
+            amp = carried(NS + 4, z)
+            flux_ref[g, NS + 4] = linear(NS + 4) + z * acoustic + amp
+            mass = acoustic + total
+            swing = sound * (faster - slower)
+            flux_ref[g, NS] = linear(NS) + vel[0] * mass + swing
+            flux_ref[g, NS + 1] = linear(NS + 1) + vel[1] * mass + shears[0]
+            flux_ref[g, NS + 2] = linear(NS + 2) + vel[2] * mass + shears[1]
+            blend = tree([a * b for a, b in zip(y, phi)])
+            flux_ref[g, NS + 3] = (
+                linear(NS + 3)
+                + tree([v * v for v in vel]) * mass
+                + ((sound * sound - blend) * acoustic - weighted) / gamma
+                + vel[0] * swing
+                + vel[1] * shears[0]
+                + vel[2] * shears[1]
+            )
+            turn_back(g - 15)
+            return 0
+
+        lax.fori_loop(first, last, step, 0)
+
     for side, first in ((0, ny - 3), (1, 0)):
         for k in range(3):
             for r in range(NVAR):
@@ -336,24 +439,51 @@
         return tuple(jnp.maximum(b, jnp.abs(v) + sound) for b, v in zip(best, vel))
 
     zero = jnp.zeros(tile, jnp.float32)
-    best = lax.fori_loop(0, 8, x_state, (zero, zero, zero))
+    best = lax.fori_loop(0, 8, x_state, (zero, zero, zero), unroll=2)
     best = [jnp.max(b, axis=(0, 1), keepdims=True) for b in best]
     column = lax.broadcasted_iota(jnp.int32, (1, lanes), 1)
     mine_ref[...] = jnp.where(column == 0, best[0], jnp.where(column == 1, best[1], best[2]))
+    def x_cells(x, _):
+        u = [own(r, x) for r in range(NVAR)]
+        state = [cache_ref[x, k] for k in range(8)]
+        cells(0, x + 3, u, (state[0], state[1:4], *state[4:]))
+        return 0
+
+    for r in range(NVAR):
+        z_ref[pl.ds(r * block, block), :] = flip(x_ref[pl.ds(r * block, block), :])
+    lax.fori_loop(0, 8, x_cells, 0)
+    own_cells(1, turned)
     pl.semaphore_wait(barrier, len(others))
 
-    peers = []
     for n, (ox, oy) in enumerate(others):
         copy = pltpu.make_async_remote_copy(
             src_ref=mine_ref,
             dst_ref=slots_ref.at[n],
-            send_sem=small_send.at[n],
-            recv_sem=small_recv.at[n],
+            send_sem=small_send,
+            recv_sem=small_recv,
             device_id=there(ox, oy),
             device_id_type=MESH,
         )
         copy.start()
-        peers.append(copy)
+    own_cells(2, upright)
+
+    lane = lax.broadcasted_iota(jnp.int32, tile, 1)
+    row = lax.broadcasted_iota(jnp.int32, tile, 0)
+    walls = kind_ref[0] == 1, kind_ref[1] == 1
+    outside = (row == 0) & (lane < block), (row == 7) & (lane >= block)
+    wrap = row == 0, row == 7
+
+    def beyond(side, r, k):
+        inner = upright(r, (7 - k) if side else (2 - k))
+        edge = upright(r, 7 if side else 0)
+        ghost = jnp.where(walls[side], -inner if r == NS + 2 else inner, edge)
+        if side:
+            along = pltpu.roll(upright(r, k), 7, 0)
+        else:
+            along = pltpu.roll(upright(r, 5 + k), 1, 0)
+        across = pltpu.roll(along, block, 1)
+        return jnp.where(outside[side], ghost, jnp.where(wrap[side], across, along))
+
     halos = []
     for n, (origin, target, device) in enumerate(
         (
@@ -374,42 +504,8 @@
         copy.start()
         halos.append(copy)
 
-    def x_cells(x, _):
-        u = [own(r, x) for r in range(NVAR)]
-        state = [cache_ref[x, k] for k in range(8)]
-        cells(0, x + 3, u, (state[0], state[1:4], *state[4:]))
-        return 0
-
-    side_by_side = lax.broadcasted_iota(jnp.int32, (block, lanes), 1) < block
-
-    def flip(a):
-        b = jnp.concatenate([a, a], axis=0).T
-        return jnp.where(side_by_side, b[:block], b[block:])
-
-    for r in range(NVAR):
-        z_ref[pl.ds(r * block, block), :] = flip(x_ref[pl.ds(r * block, block), :])
-    lax.fori_loop(0, 8, x_cells, 0)
-    own_cells(1, turned)
-    own_cells(2, upright)
-
-    lane = lax.broadcasted_iota(jnp.int32, tile, 1)
-    row = lax.broadcasted_iota(jnp.int32, tile, 0)
-    walls = kind_ref[0] == 1, kind_ref[1] == 1
-    outside = (row == 0) & (lane < block), (row == 7) & (lane >= block)
-    wrap = row == 0, row == 7
-
-    def beyond(side, r, k):
-        inner = upright(r, (7 - k) if side else (2 - k))
-        edge = upright(r, 7 if side else 0)
-        ghost = jnp.where(walls[side], -inner if r == NS + 2 else inner, edge)
-        if side:
-            along = pltpu.roll(upright(r, k), 7, 0)
-        else:
-            along = pltpu.roll(upright(r, 5 + k), 1, 0)
-        across = pltpu.roll(along, block, 1)
-        return jnp.where(outside[side], ghost, jnp.where(wrap[side], across, along))
-
-    halo_cells(2, beyond)
+    for side in range(2):
+        halo_cells(2, side, beyond)
     differences(0, 3, 10)
     differences(1, 3, 10)
     differences(2, 0, 13)
@@ -417,8 +513,8 @@
     project(1, 3, 6, 9)
     project(0, 3, 6, 12)
 
-    for copy in peers:
-        copy.wait()
+    for sem in (small_recv, small_send):
+        pltpu.make_async_copy(slots_ref, slots_ref, sem).wait()
     value = mine_ref[...]
     for n in range(len(others)):
         value = jnp.maximum(value, slots_ref[n])
@@ -428,22 +524,9 @@
         )
         for d in range(3)
     ]
-    for g in range(3 * FACES):
-        alpha_ref[g] = alphas[2 if g < 9 else 1 if g < 12 or 15 <= g < 21 else 0]
-
-    advance(0, 15)
-    for d, read, pair, start in (
-        (1, lambda side, r, k: hy_ref[side, k, r], halos[2:], 15),
-        (0, lambda side, r, k: hx_ref[side, r, k], halos[:2], 21),
-    ):
-        for copy in pair:
-            copy.wait()
-        halo_cells(d, read)
-        differences(d, 0, 3)
-        differences(d, 10, 13)
-        project(d, 0, 3, start)
-        project(d, 6, 9, start + 3)
-        advance(start, start + 6)
+    for g in range(15):
+        alpha_ref[g] = alphas[2 if g < 9 else 1 if g < 12 else 0]
+    scale = (-COURANT / 6.0) / (alphas[0] + alphas[1] + alphas[2])
 
     def slot(d, i):
         if d == 2:
@@ -452,22 +535,33 @@
             return (9 if d else 12) + i - 3
         return (15 if d else 21) + (i if i < 3 else i - 3)
 
-    scale = (-COURANT / 6.0) / (alphas[0] + alphas[1] + alphas[2])
-
     def rate(d, i, r):
         n = NS + ORDER[d].index(r - NS) if NS <= r < NS + 3 else r
         return flux_ref[slot(d, i + 1), n] - flux_ref[slot(d, i), n]
 
+    advance(0, 15)
+    for r in range(NVAR):
+        for i in range(8):
+            back_ref[pl.ds(r * block + i, 8, stride=8), :] = rate(2, i, r)
+    for d, read, pair, start in (
+        (1, lambda side, r, k: hy_ref[side, k, r], halos[2:], 15),
+        (0, lambda side, r, k: hx_ref[side, r, k], halos[:2], 21),
+    ):
+        split_inner(d)
+        for side, copy in enumerate(pair):
+            copy.wait()
+            halo_cells(d, side, read)
+            split_outer(d, 10 * side)
+            direct(d, 6 * side, 6 * side + 3, start + 3 * side)
+    for r in range(12, NVAR):
+        turn_back(r)
     for r in range(NVAR):
         for i in range(8):
             acc_ref[pl.ds(r * block + i, 8, stride=8), :] = rate(1, i, r)
-            back_ref[pl.ds(r * block + i, 8, stride=8), :] = rate(2, i, r)
-        back = flip(back_ref[pl.ds(r * block, block), :])
+    for r in range(NVAR):
         for i in range(8):
             rows = pl.ds(r * block + i * 8, 8)
-            out_ref[rows, :] = scale * (
-                rate(0, i, r) + acc_ref[rows, :] + back[i * 8 : i * 8 + 8]
-            )
+            out_ref[rows, :] = scale * (rate(0, i, r) + acc_ref[rows, :] + back_ref[rows, :])
 
 
 def shards(preserved_vector, nasa_table, gas_constant, species_index, face_kind):
@@ -504,14 +598,16 @@
             buffer(3, 14, NVAR + 1),
             buffer(3, 13, NVAR + 1),
             buffer(3, 13, NVAR + 1),
-            buffer(3 * FACES, NVAR * ROW),
-            buffer(3 * FACES, COEFS),
-            buffer(3 * FACES),
+            buffer(15, NVAR * ROW),
+            buffer(15, COEFS),
+            buffer(15),
             buffer(3 * FACES, NVAR),
+            buffer(2, 13, NVAR + 1),
+            buffer(2, 13, NVAR + 1),
             dma(()),
             dma((4,)),
-            dma((others,)),
-            dma((others,)),
+            dma(()),
+            dma(()),
             dma((4,)),
             dma((4,)),
         ],

time: 22.1 us -> 19.6 us (0.89)
  Pallas kernels: 21.2 us -> 18.7 us
    pallas_call x1, Pallas kernels: 21.2 us -> 18.7 us  [shards(): pl.pallas_call(functools.partial(fused, size_x, size_y), out_shape=pltpu....]
where the time goes in v3:
time: 19.6 us; the launch traced here: 19.5 us
  Pallas kernels  18.7 us (95%)
  local copies, waits for them, and re-layouts  0.77 us (4%)
    pallas_call x1, Pallas kernels, shards(): pl.pallas_call(functools.partial(fused, size_x, size_y), out_shape=pltpu....  18.7 us
    unnamed x1, local copies, waits for them, and re-layouts  0.77 us

profile of v3, /device:TPU:0, one launch (start us, length us, event | category | flops | bytes accessed | tf_op | source)
XLA Modules:
  0.0 19.5 jit_solution(1744255653501423107)
XLA Ops:
  0.0 18.7 %increment.1 = f32[896,128]{1,0:T(8,128)S(1)} custom-call(f32[6,32]{1,0:T(8,128)} %bitcast.6, f32[32]{0:T(128)} %gas_hbm.1, s32[9]{0:T(128)} %index_hbm.1, s32[2]{0:T(128)} %bitcast.7, f32[896,128]{1,0:T(8,128)} %bitcast.5, f32[14,8,8,128]{3,2,1,0:T(8,128)} %planes_ref.1), custom_call_target="tpu_custom_call" | custom-call | tf_op jit(solution)/shard_map/increment/pallas_call | solution.py:578
  18.7 0.8 %copy.7 = f32[14,8,8,128]{3,2,1,0:T(8,128)} copy(f32[14,8,8,128]{3,2,1,0:T(8,128)S(1)} %bitcast.4) | data formatting | bytes 917504

commit v4 on v3

--- a/solution.py
+++ b/solution.py
@@ -71,13 +71,14 @@
     return inverse, vel, temp, pressure, gamma, sound
 
 
-def slopes_of(temp, gamma, square, table_ref):
-    kinetic = 0.5 * gamma * square
+def half_slopes(temp, gamma, vel, table_ref):
+    warm, lean = 0.5 * temp, 0.5 * gamma
+    kinetic = (0.5 * lean) * tree([v * v for v in vel])
     result = []
     for i in range(NS):
         k = [table_ref[n * NS + i] for n in range(7)]
         e = k[1] + temp * (k[2] + temp * (k[3] + temp * (k[4] + temp * (k[5] + temp * k[6]))))
-        result.append(k[0] * temp - gamma * e + kinetic)
+        result.append(k[0] * warm - lean * e + kinetic)
     return result
 
 
@@ -104,7 +105,7 @@
     nasa_ref, gas_ref, index_ref, kind_ref,
     x_ref, z_ref, acc_ref, back_ref, hx_ref, sy_ref, hy_ref, mine_ref, slots_ref,
     table_ref, cache_ref, prim_ref, f_ref, u_ref, df_ref, du_ref,
-    part_ref, coef_ref, alpha_ref, flux_ref, up_ref, down_ref,
+    part_ref, coef_ref, flux_ref, up_ref, down_ref,
     load_sem, param_sem, small_send, small_recv, big_send, big_recv,
 ):
     load = pltpu.make_async_copy(flat_ref, x_ref, load_sem)
@@ -170,15 +171,15 @@
         inverse, vel, temp, pressure, gamma, sound = state
         flow(d, p, u, vel, pressure)
         q = p - 2
+        share = 0.5 * inverse
         for k in range(NS):
-            prim_ref[d, q, k] = u[k] * inverse
+            prim_ref[d, q, k] = u[k] * share
         for k in range(3):
-            prim_ref[d, q, VEL + k] = vel[ORDER[d][k]]
-        prim_ref[d, q, PASSIVE] = u[NS + 4] * inverse
-        prim_ref[d, q, GAMMA] = gamma
-        prim_ref[d, q, SOUND] = sound
-        square = tree([v * v for v in vel])
-        for k, value in enumerate(slopes_of(temp, gamma, square, table_ref)):
+            prim_ref[d, q, VEL + k] = 0.5 * vel[ORDER[d][k]]
+        prim_ref[d, q, PASSIVE] = u[NS + 4] * share
+        prim_ref[d, q, GAMMA] = 0.5 * gamma
+        prim_ref[d, q, SOUND] = 0.5 * sound
+        for k, value in enumerate(half_slopes(temp, gamma, vel, table_ref)):
             prim_ref[d, q, SLOPES + k] = value
 
     def own_cells(d, read):
@@ -231,12 +232,27 @@
 
     def means(d, i):
         def mean(q):
-            return 0.5 * (prim_ref[d, i, q] + prim_ref[d, i + 1, q])
+            return prim_ref[d, i, q] + prim_ref[d, i + 1, q]
 
         y = [mean(k) for k in range(NS)]
         vel = [mean(VEL + k) for k in range(3)]
         phi = [mean(SLOPES + k) for k in range(NS)]
         return y, vel, phi, mean(PASSIVE), mean(GAMMA), mean(SOUND)
+
+    def keep_means(d, i, g):
+        y, vel, phi, z, gamma, sound = means(d, i)
+        inv = 1.0 / sound
+        steep = 1.0 / gamma
+        for k in range(NS):
+            coef_ref[g, k] = y[k]
+            coef_ref[g, STEEP + k] = phi[k] * steep
+        for k in range(3):
+            coef_ref[g, VEL + k] = vel[k]
+        coef_ref[g, PASSIVE] = z
+        coef_ref[g, GAMMA] = sound
+        coef_ref[g, ENTHALPY] = (sound * sound - tree([a * b for a, b in zip(y, phi)])) * steep
+        coef_ref[g, SQUARE] = tree([v * v for v in vel])
+        return y, vel, phi, z, gamma, inv * inv, 0.5 * inv
 
     def waves_of(get, vel, phi, gamma, inv2, half_inv):
         s = get(TOTAL)
@@ -252,21 +268,7 @@
     def project(d, first, last, start):
         def step(i, _):
             g = i + (start - first)
-            y, vel, phi, z, gamma, sound = means(d, i)
-            inv = 1.0 / sound
-            inv2, half_inv = inv * inv, 0.5 * inv
-            steep = 1.0 / gamma
-            for k in range(NS):
-                coef_ref[g, k] = y[k]
-                coef_ref[g, STEEP + k] = phi[k] * steep
-            for k in range(3):
-                coef_ref[g, VEL + k] = vel[k]
-            coef_ref[g, PASSIVE] = z
-            coef_ref[g, GAMMA] = sound
-            coef_ref[g, ENTHALPY] = (
-                sound * sound - tree([a * b for a, b in zip(y, phi)])
-            ) * steep
-            coef_ref[g, SQUARE] = tree([v * v for v in vel])
+            y, vel, phi, z, gamma, inv2, half_inv = keep_means(d, i, g)
             for half, ref in enumerate((df_ref, du_ref)):
 
                 def keep(n, d5):
@@ -297,9 +299,35 @@
 
         lax.fori_loop(first, last, step, 0)
 
-    def advance(first, last):
+    def combine(d, g, c, wave, linear):
+        slower, faster = wave(NS), wave(NS + 3)
+        shears = [wave(NS + 1), wave(NS + 2)]
+        acoustic = slower + faster
+        total, weighted = None, None
+        for n in range(NS):
+            amp = wave(n)
+            flux_ref[g, n] = linear(n) + coef_ref[c, n] * acoustic + amp
+            steep = coef_ref[c, STEEP + n] * amp
+            total = amp if n == 0 else total + amp
+            weighted = steep if n == 0 else weighted + steep
+        amp = wave(NS + 4)
+        flux_ref[g, NS + 4] = linear(NS + 4) + coef_ref[c, PASSIVE] * acoustic + amp
+        mass = acoustic + total
+        swing = coef_ref[c, GAMMA] * (faster - slower)
+        vel = [coef_ref[c, VEL + n] for n in range(3)]
+        moved = [swing] + shears
+        for n, r in enumerate(ORDER[d]):
+            flux_ref[g, NS + r] = linear(NS + n) + vel[n] * mass + moved[n]
+        flux_ref[g, NS + 3] = (
+            linear(NS + 3)
+            + coef_ref[c, SQUARE] * mass
+            + (coef_ref[c, ENTHALPY] * acoustic - weighted)
+            + tree([v * m for v, m in zip(vel, moved)])
+        )
+
+    def advance(d, first, last):
         def step(g, _):
-            alpha = alpha_ref[g]
+            alpha = alphas[d]
 
             def wave(n):
                 f = [part_ref[g, n * ROW + j] for j in range(PARTS)]
@@ -312,32 +340,7 @@
                 at = n * ROW + 2 * PARTS
                 return part_ref[g, at] + alpha * part_ref[g, at + 1]
 
-            slower, faster = wave(NS), wave(NS + 3)
-            shears = [wave(NS + 1), wave(NS + 2)]
-            acoustic = slower + faster
-            total, weighted = None, None
-            for n in range(NS):
-                amp = wave(n)
-                flux_ref[g, n] = linear(n) + coef_ref[g, n] * acoustic + amp
-                steep = coef_ref[g, STEEP + n] * amp
-                total = amp if n == 0 else total + amp
-                weighted = steep if n == 0 else weighted + steep
-            amp = wave(NS + 4)
-            flux_ref[g, NS + 4] = linear(NS + 4) + coef_ref[g, PASSIVE] * acoustic + amp
-            mass = acoustic + total
-            swing = coef_ref[g, GAMMA] * (faster - slower)
-            vel = [coef_ref[g, VEL + n] for n in range(3)]
-            flux_ref[g, NS] = linear(NS) + vel[0] * mass + swing
-            flux_ref[g, NS + 1] = linear(NS + 1) + vel[1] * mass + shears[0]
-            flux_ref[g, NS + 2] = linear(NS + 2) + vel[2] * mass + shears[1]
-            flux_ref[g, NS + 3] = (
-                linear(NS + 3)
-                + coef_ref[g, SQUARE] * mass
-                + (coef_ref[g, ENTHALPY] * acoustic - weighted)
-                + vel[0] * swing
-                + vel[1] * shears[0]
-                + vel[2] * shears[1]
-            )
+            combine(d, g, g, wave, linear)
             return 0
 
         lax.fori_loop(first, last, step, 0)
@@ -350,44 +353,57 @@
 
     def turn_back(r):
         rows = pl.ds(pl.multiple_of(r * block, block), block)
-        back_ref[rows, :] = flip(back_ref[rows, :])
-
-    def direct(d, first, last, start):
-        def step(i, _):
-            g = i + (start - first)
-            y, vel, phi, z, gamma, sound = means(d, i)
-            inv = 1.0 / sound
-            inv2, half_inv = inv * inv, 0.5 * inv
-
-            def rising(n, k):
-                return up_ref[d, i + k, n]
-
-            def falling(n, k):
-                return down_ref[d, i + 4 - k, n]
-
-            sides = [
-                [
-                    waves_of(lambda n: get(n, k), vel, phi, gamma, inv2, half_inv)
-                    for k in range(4)
-                ]
-                for get in (rising, falling)
-            ]
-
-            def both(up, down):
-                pair = [
-                    correction(v[1], v[2], v[1] - v[0], v[2] - v[1], v[3] - v[2])
-                    for v in (up, down)
-                ]
+        z_ref[rows, :] = flip(back_ref[rows, :])
+
+    def slot(d, i):
+        if d == 2:
+            return i
+        if 3 <= i < 6:
+            return (9 if d else 12) + i - 3
+        return (15 if d else 21) + (i if i < 3 else i - 3)
+
+    def rate(d, i, r):
+        return flux_ref[slot(d, i + 1), r] - flux_ref[slot(d, i), r]
+
+    def gather_y(r):
+        for i in range(8):
+            acc_ref[pl.ds(r * block + i, 8, stride=8), :] = rate(1, i, r)
+
+    def outer_face(h):
+        return jnp.where(h < 3, h, h + 3)
+
+    def lay(d, first, last):
+        def step(h, _):
+            i = outer_face(h)
+            y, vel, phi, z, gamma, inv2, half_inv = keep_means(d, i, h)
+            for side, get in enumerate(
+                (
+                    lambda n, k: up_ref[d, i + k, n],
+                    lambda n, k: down_ref[d, i + 4 - k, n],
+                )
+            ):
+                for k in range(4):
+                    at = 4 * side + k
+                    waves = waves_of(lambda n: get(n, k), vel, phi, gamma, inv2, half_inv)
+                    for n in range(4):
+                        part_ref[h, (NS + n) * 8 + at] = waves[n + 1]
+                    for n in range(NS):
+                        part_ref[h, n * 8 + at] = get(n, k) - y[n] * waves[0]
+                    part_ref[h, (NS + 4) * 8 + at] = get(NS + 4, k) - z * waves[0]
+            return 0
+
+        lax.fori_loop(first, last, step, 0)
+
+    def close(d, first, last):
+        def step(h, _):
+            i = outer_face(h)
+
+            def wave(n):
+                pair = []
+                for side in range(2):
+                    v = [part_ref[h, n * 8 + side * 4 + k] for k in range(4)]
+                    pair.append(correction(v[1], v[2], v[1] - v[0], v[2] - v[1], v[3] - v[2]))
                 return pair[0] - pair[1]
-
-            def wave(n):
-                return both(*[[w[n] for w in side] for side in sides])
-
-            def carried(n, share):
-                return both(
-                    [rising(n, k) - share * sides[0][k][0] for k in range(4)],
-                    [falling(n, k) - share * sides[1][k][0] for k in range(4)],
-                )
 
             def linear(n):
                 ahead = up_ref[d, i + 2, n] - down_ref[d, i + 2, n]
@@ -395,33 +411,10 @@
                     (up_ref[d, i + 1, n] - down_ref[d, i + 3, n]) - ahead
                 )
 
-            slower, faster = wave(1), wave(4)
-            shears = [wave(2), wave(3)]
-            acoustic = slower + faster
-            total, weighted = None, None
-            for n in range(NS):
-                amp = carried(n, y[n])
-                flux_ref[g, n] = linear(n) + y[n] * acoustic + amp
-                term = phi[n] * amp
-                total = amp if n == 0 else total + amp
-                weighted = term if n == 0 else weighted + term
-            amp = carried(NS + 4, z)
-            flux_ref[g, NS + 4] = linear(NS + 4) + z * acoustic + amp
-            mass = acoustic + total
-            swing = sound * (faster - slower)
-            flux_ref[g, NS] = linear(NS) + vel[0] * mass + swing
-            flux_ref[g, NS + 1] = linear(NS + 1) + vel[1] * mass + shears[0]
-            flux_ref[g, NS + 2] = linear(NS + 2) + vel[2] * mass + shears[1]
-            blend = tree([a * b for a, b in zip(y, phi)])
-            flux_ref[g, NS + 3] = (
-                linear(NS + 3)
-                + tree([v * v for v in vel]) * mass
-                + ((sound * sound - blend) * acoustic - weighted) / gamma
-                + vel[0] * swing
-                + vel[1] * shears[0]
-                + vel[2] * shears[1]
-            )
-            turn_back(g - 15)
+            combine(d, h + (15 if d else 21), h, wave, linear)
+            if d:
+                for k in range(3):
+                    turn_back(jnp.minimum(3 * h + k, NVAR - 1))
             return 0
 
         lax.fori_loop(first, last, step, 0)
@@ -452,7 +445,6 @@
     for r in range(NVAR):
         z_ref[pl.ds(r * block, block), :] = flip(x_ref[pl.ds(r * block, block), :])
     lax.fori_loop(0, 8, x_cells, 0)
-    own_cells(1, turned)
     pl.semaphore_wait(barrier, len(others))
 
     for n, (ox, oy) in enumerate(others):
@@ -465,6 +457,7 @@
             device_id_type=MESH,
         )
         copy.start()
+    own_cells(1, turned)
     own_cells(2, upright)
 
     lane = lax.broadcasted_iota(jnp.int32, tile, 1)
@@ -515,53 +508,44 @@
 
     for sem in (small_recv, small_send):
         pltpu.make_async_copy(slots_ref, slots_ref, sem).wait()
-    value = mine_ref[...]
-    for n in range(len(others)):
-        value = jnp.maximum(value, slots_ref[n])
+    value = jnp.maximum(mine_ref[...], jnp.max(slots_ref[...], axis=0))
     alphas = [
         jnp.broadcast_to(
             jnp.max(jnp.where(column == d, value, 0.0), axis=1, keepdims=True), tile
         )
         for d in range(3)
     ]
-    for g in range(15):
-        alpha_ref[g] = alphas[2 if g < 9 else 1 if g < 12 else 0]
     scale = (-COURANT / 6.0) / (alphas[0] + alphas[1] + alphas[2])
 
-    def slot(d, i):
-        if d == 2:
-            return i
-        if 3 <= i < 6:
-            return (9 if d else 12) + i - 3
-        return (15 if d else 21) + (i if i < 3 else i - 3)
-
-    def rate(d, i, r):
-        n = NS + ORDER[d].index(r - NS) if NS <= r < NS + 3 else r
-        return flux_ref[slot(d, i + 1), n] - flux_ref[slot(d, i), n]
-
-    advance(0, 15)
+    advance(2, 0, 9)
+    advance(1, 9, 12)
+    advance(0, 12, 15)
+    for copy in halos[2:]:
+        copy.wait()
     for r in range(NVAR):
         for i in range(8):
             back_ref[pl.ds(r * block + i, 8, stride=8), :] = rate(2, i, r)
-    for d, read, pair, start in (
-        (1, lambda side, r, k: hy_ref[side, k, r], halos[2:], 15),
-        (0, lambda side, r, k: hx_ref[side, r, k], halos[:2], 21),
-    ):
-        split_inner(d)
-        for side, copy in enumerate(pair):
-            copy.wait()
-            halo_cells(d, side, read)
-            split_outer(d, 10 * side)
-            direct(d, 6 * side, 6 * side + 3, start + 3 * side)
-    for r in range(12, NVAR):
-        turn_back(r)
-    for r in range(NVAR):
-        for i in range(8):
-            acc_ref[pl.ds(r * block + i, 8, stride=8), :] = rate(1, i, r)
+    for side in range(2):
+        halo_cells(1, side, lambda side, r, k: hy_ref[side, k, r])
+    split_inner(1)
+    split_outer(1, 0)
+    split_outer(1, 10)
+    lay(1, 0, 6)
+    close(1, 0, 6)
+    split_inner(0)
+    for side, copy in enumerate(halos[:2]):
+        copy.wait()
+        for r in range(NVAR):
+            if r % 2 == side:
+                gather_y(r)
+        halo_cells(0, side, lambda side, r, k: hx_ref[side, r, k])
+        split_outer(0, 10 * side)
+        lay(0, 3 * side, 3 * side + 3)
+        close(0, 3 * side, 3 * side + 3)
     for r in range(NVAR):
         for i in range(8):
             rows = pl.ds(r * block + i * 8, 8)
-            out_ref[rows, :] = scale * (rate(0, i, r) + acc_ref[rows, :] + back_ref[rows, :])
+            out_ref[rows, :] = scale * (rate(0, i, r) + acc_ref[rows, :] + z_ref[rows, :])
 
 
 def shards(preserved_vector, nasa_table, gas_constant, species_index, face_kind):
@@ -600,7 +584,6 @@
             buffer(3, 13, NVAR + 1),
             buffer(15, NVAR * ROW),
             buffer(15, COEFS),
-            buffer(15),
             buffer(3 * FACES, NVAR),
             buffer(2, 13, NVAR + 1),
             buffer(2, 13, NVAR + 1),

time: 19.6 us -> 19.6 us (level)
  no operation moved by 1% of the time
where the time goes in v4:
time: 19.6 us; the launch traced here: 19.4 us
  Pallas kernels  18.6 us (95%)
  local copies, waits for them, and re-layouts  0.77 us (4%)
    pallas_call x1, Pallas kernels, shards(): pl.pallas_call(functools.partial(fused, size_x, size_y), out_shape=pltpu....  18.6 us
    unnamed x1, local copies, waits for them, and re-layouts  0.77 us

profile of v4, /device:TPU:0, one launch (start us, length us, event | category | flops | bytes accessed | tf_op | source)
XLA Modules:
  0.0 19.4 jit_solution(3669109352690543824)
XLA Ops:
  0.0 18.6 %increment.1 = f32[896,128]{1,0:T(8,128)S(1)} custom-call(f32[6,32]{1,0:T(8,128)} %bitcast.6, f32[32]{0:T(128)} %gas_hbm.1, s32[9]{0:T(128)} %index_hbm.1, s32[2]{0:T(128)} %bitcast.7, f32[896,128]{1,0:T(8,128)} %bitcast.5, f32[14,8,8,128]{3,2,1,0:T(8,128)} %planes_ref.1), custom_call_target="tpu_custom_call" | custom-call | tf_op jit(solution)/shard_map/increment/pallas_call | solution.py:562
  18.6 0.8 %copy.7 = f32[14,8,8,128]{3,2,1,0:T(8,128)} copy(f32[14,8,8,128]{3,2,1,0:T(8,128)S(1)} %bitcast.4) | data formatting | bytes 917504

commit v5 on v4

--- a/solution.py
+++ b/solution.py
@@ -343,7 +343,7 @@
             combine(d, g, g, wave, linear)
             return 0
 
-        lax.fori_loop(first, last, step, 0)
+        lax.fori_loop(first, last, step, 0, unroll=3)
 
     side_by_side = lax.broadcasted_iota(jnp.int32, (block, lanes), 1) < block
 
@@ -392,7 +392,7 @@
                     part_ref[h, (NS + 4) * 8 + at] = get(NS + 4, k) - z * waves[0]
             return 0
 
-        lax.fori_loop(first, last, step, 0)
+        lax.fori_loop(first, last, step, 0, unroll=3)
 
     def close(d, first, last):
         def step(h, _):
@@ -417,7 +417,7 @@
                     turn_back(jnp.minimum(3 * h + k, NVAR - 1))
             return 0
 
-        lax.fori_loop(first, last, step, 0)
+        lax.fori_loop(first, last, step, 0, unroll=3)
 
     for side, first in ((0, ny - 3), (1, 0)):
         for k in range(3):

time: 19.6 us -> 19.4 us (0.990)
  no operation moved by 1% of the time
where the time goes in v5:
time: 19.4 us; the launch traced here: 19.3 us
  Pallas kernels  18.5 us (95%)
  local copies, waits for them, and re-layouts  0.77 us (4%)
    pallas_call x1, Pallas kernels, shards(): pl.pallas_call(functools.partial(fused, size_x, size_y), out_shape=pltpu....  18.5 us
    unnamed x1, local copies, waits for them, and re-layouts  0.77 us

profile of v5, /device:TPU:0, one launch (start us, length us, event | category | flops | bytes accessed | tf_op | source)
XLA Modules:
  0.0 19.3 jit_solution(4477524076877938237)
XLA Ops:
  0.0 18.5 %increment.1 = f32[896,128]{1,0:T(8,128)S(1)} custom-call(f32[6,32]{1,0:T(8,128)} %bitcast.6, f32[32]{0:T(128)} %gas_hbm.1, s32[9]{0:T(128)} %index_hbm.1, s32[2]{0:T(128)} %bitcast.7, f32[896,128]{1,0:T(8,128)} %bitcast.5, f32[14,8,8,128]{3,2,1,0:T(8,128)} %planes_ref.1), custom_call_target="tpu_custom_call" | custom-call | tf_op jit(solution)/shard_map/increment/pallas_call | solution.py:562
  18.5 0.8 %copy.7 = f32[14,8,8,128]{3,2,1,0:T(8,128)} copy(f32[14,8,8,128]{3,2,1,0:T(8,128)S(1)} %bitcast.4) | data formatting | bytes 917504
